TPU v7x, 256 devices: a whole 4x4x8 slice. The times are simulated.
256 devices in a mesh: tm: 2 (over core), space: 128 (over z, y, x).
Axes of the slice: x: 4, y: 4, z: 8, core: 2. Of those that a mesh axis runs over, the one named last changes fastest.
Arguments:
- checkpoints: float32 [2, 5, 16384, 128], P('tm', None, 'space'), may hold values from -6 to 6
- sources: float32 [2, 5, 16384, 128], P(None, None, 'space'), may hold values from -3 to 3
- pitch: float32 [8], replicated, may hold values from -3.140625 to 3.140625
- metric: float32 [16384, 128], P('space'), may hold values from 0.5 to 2
- obj_weight: float32 [5, 16384, 128], P(None, 'space'), may hold values from 0.1 to 0.6
- adjoint_end: float32 [5, 16384, 128], P(None, 'space'), may hold values from -6 to 6
- lift: bfloat16 [5, 128, 128], replicated, may hold values from -0.5 to 0.5
- mixing: float32 [5, 5, 5], replicated, may hold values from -1.25 to 1.25
- faces: int32 [16384, 4], P('space'), may hold values from 0 to 191
- send_idx: int32 [128, 4, 16], P('space'), may hold values from 0 to 127
Outputs:
- adjoint_bounds: float32 [2, 5, 16384, 128], P('tm', None, 'space')
- pitch_grad: float32 [8], replicated
Inputs may be any that keep to these rules, and one draw needn't show every extreme that they name: `faces`: values below 128 name the subdomain's own blocks; value 128 + d * 16 + s names slot s of the blocks received from direction d. `send_idx`: entry [p, d, s] is a local block of subdomain p sent to subdomain p + o[d], o = (1, -1, 2, -2); blocks may repeat.
All inputs are finite; a program needn't handle non-finite values.
Results may differ from a plain program's by a relative error of at most 0.0035.
Values may be sent and summed in bfloat16 or wider, within the bound.
A program may use at most 64 MiB of HBM per device.

v0:
```python
import functools
import math

import jax
import jax.numpy as jnp
from jax import lax
from jax.experimental import pallas as pl
from jax.experimental.pallas import tpu as pltpu
from jax.sharding import PartitionSpec as P

OFFSETS = (1, -1, 2, -2)
STEP_SIZE = 0.5
MESH = pl.DeviceIdType.MESH
F32, BF16 = jnp.float32, jnp.bfloat16
CHUNK = 32


def matmul(left, right):
    return jnp.dot(left, right, preferred_element_type=F32)


def sweep(
    n_space,
    plane,
    checkpoint_in,
    sources_in,
    pitch,
    metric_in,
    weight_in,
    end_in,
    lift_in,
    mixing,
    faces,
    send_idx,
    bounds,
    grads,
    states,
    sources,
    metric,
    weight,
    adjoint,
    kept,
    lift,
    lift_t,
    cosines,
    sines,
    pick,
    pick_t,
    near,
    near_t,
    far,
    far_t,
    squashed,
    gathered,
    lifted,
    base,
    slope,
    halo_lifted,
    halo_mixed,
    split,
    pulled,
    halo_pulled,
    mixed,
    far_mixed,
    fwd_out,
    fwd_in,
    rev_out,
    rev_in,
    partial,
    plane_parts,
    plane_sum,
    layer_parts,
    in_sem,
    fwd_send,
    fwd_recv,
    rev_send,
    rev_recv,
    state_send,
    state_recv,
    plane_send,
    plane_recv,
    layer_send,
    layer_recv,
    end_sem,
    out_sem,
):
    comps, blocks, nodes = states.shape[1:]
    slots = lift.shape[0]
    halo = fwd_in.shape[2]
    ghosts = 4 * halo
    levels = pitch.shape[0]
    half = levels // 2
    layers = n_space // plane
    t = lax.axis_index("tm")
    p = lax.axis_index("space")
    spot = lax.rem(p, plane)
    layer = p // plane
    first = t * half

    def exists(q):
        return jnp.logical_and(q >= 0, q < n_space)

    def lane(c):
        return slice(c * nodes, (c + 1) * nodes)

    loads = [
        pltpu.make_async_copy(checkpoint_in.at[0], states.at[first], in_sem.at[0]),
        pltpu.make_async_copy(lift_in, lift, in_sem.at[1]),
        pltpu.make_async_copy(metric_in, metric, in_sem.at[2]),
        pltpu.make_async_copy(sources_in, sources, in_sem.at[3]),
        pltpu.make_async_copy(weight_in, weight, in_sem.at[4]),
        pltpu.make_async_copy(end_in, adjoint, in_sem.at[5]),
    ]
    for load in loads:
        load.start()

    barrier = pltpu.get_barrier_semaphore()

    def greet(device):
        pl.semaphore_signal(barrier, inc=1, device_id=device, device_id_type=MESH)

    for offset in OFFSETS:

        @pl.when(exists(p + offset))
        def _():
            greet((t, p + offset))

    greet((1 - t, p))
    for r in range(1, layers):
        greet((1, lax.rem(layer + r, layers) * plane + spot))

    @pl.when(t == 1)
    def _():
        for r in range(1, plane):
            greet((1, layer * plane + lax.rem(spot + r, plane)))

    lane_of = lax.broadcasted_iota(jnp.int32, (1, blocks), 1)
    for d in range(4):
        for s in range(halo):
            row = d * halo + s
            pick[pl.ds(row, 1), :] = jnp.where(lane_of == send_idx[0, d, s], 1.0, 0.0)

    for d, offset in enumerate(OFFSETS):

        @pl.when(jnp.logical_not(exists(p - offset)))
        def _():
            for i in range(half):
                fwd_in[i, d] = jnp.zeros(fwd_in.shape[2:], BF16)

        @pl.when(jnp.logical_not(exists(p + offset)))
        def _():
            for i in range(levels):
                rev_in[i, d] = jnp.zeros(rev_in.shape[2:], BF16)

    def fwd_copy(i, d, device):
        return pltpu.make_async_remote_copy(
            src_ref=fwd_out.at[i, d],
            dst_ref=fwd_in.at[i, d],
            send_sem=fwd_send.at[i, d],
            recv_sem=fwd_recv.at[i, d],
            device_id=(t, device),
            device_id_type=MESH,
        )

    def rev_copy(i, d, device):
        return pltpu.make_async_remote_copy(
            src_ref=rev_out.at[i, d],
            dst_ref=rev_in.at[i, d],
            send_sem=rev_send.at[i, d],
            recv_sem=rev_recv.at[i, d],
            device_id=(t, device),
            device_id_type=MESH,
        )

    def state_copy(i):
        return pltpu.make_async_remote_copy(
            src_ref=states.at[i],
            dst_ref=states.at[i],
            send_sem=state_send.at[i],
            recv_sem=state_recv.at[i],
            device_id=(1 - t, p),
            device_id_type=MESH,
        )

    def plane_copy(r):
        return pltpu.make_async_remote_copy(
            src_ref=partial,
            dst_ref=plane_parts.at[spot],
            send_sem=plane_send.at[r],
            recv_sem=plane_recv.at[spot],
            device_id=(1, layer * plane + lax.rem(spot + r, plane)),
            device_id_type=MESH,
        )

    def layer_copy(r, core):
        return pltpu.make_async_remote_copy(
            src_ref=plane_sum,
            dst_ref=layer_parts.at[layer],
            send_sem=layer_send.at[core, r],
            recv_sem=layer_recv.at[layer],
            device_id=(core, lax.rem(layer + r, layers) * plane + spot),
            device_id_type=MESH,
        )

    end_copy = pltpu.make_async_remote_copy(
        src_ref=adjoint,
        dst_ref=bounds.at[0],
        send_sem=end_sem.at[0],
        recv_sem=end_sem.at[1],
        device_id=(1 - t, p),
        device_id_type=MESH,
    )
    keep_copy = pltpu.make_async_copy(kept, bounds.at[0], out_sem)

    def squash(state):
        for c in range(comps):
            squashed[:, lane(c)] = jnp.tanh(state(c)).astype(BF16)

    def send_forward(i):
        packets = matmul(pick[...].astype(BF16), squashed[...]).astype(BF16)
        for d, offset in enumerate(OFFSETS):
            fwd_out[i, d] = packets[d * halo : (d + 1) * halo]

            @pl.when(exists(p + offset))
            def _():
                fwd_copy(i, d, p + offset).start()

    def forward_near(i):
        gathered[...] = matmul(near[...], squashed[...]).astype(BF16)
        for k in range(slots):
            rows = squashed if k == 0 else gathered.at[pl.ds((k - 1) * blocks, blocks)]
            left = jnp.concatenate([rows[:, lane(c)] for c in range(comps)], axis=0)
            lifted[k] = matmul(left, lift_t[:, lane(k)])
        cosine = cosines[pl.ds(first + i, 1), :]
        sine = sines[pl.ds(first + i, 1), :]
        for start in range(0, blocks, CHUNK):
            some = slice(start, start + CHUNK)
            totals = [None] * comps
            for k in range(slots):
                for c in range(comps):
                    term = lifted[k, c * blocks + start : c * blocks + start + CHUNK, :]
                    for e in range(comps):
                        more = mixing[k, e, c] * term
                        totals[e] = more if totals[e] is None else totals[e] + more
            for e in range(comps):
                forcing = cosine * sources[0, e, some, :] + sine * sources[1, e, some, :]
                change = forcing - metric[some, :] * totals[e]
                base[e, some, :] = states[first + i, e, some, :] + STEP_SIZE * change

    def forward_far(i):
        for d, offset in enumerate(OFFSETS):

            @pl.when(exists(p - offset))
            def _():
                fwd_copy(i, d, p).wait_recv()

        ghost = jnp.concatenate([fwd_in[i, d] for d in range(4)], axis=0)
        left = jnp.concatenate([ghost[:, lane(c)] for c in range(comps)], axis=0)
        halo_lifted[...] = matmul(left, lift_t[:, nodes:])
        for k in range(1, slots):
            for start in range(0, ghosts, CHUNK):
                totals = [None] * comps
                for c in range(comps):
                    term = halo_lifted[c * ghosts + start : c * ghosts + start + CHUNK, lane(k - 1)]
                    for e in range(comps):
                        more = mixing[k, e, c] * term
                        totals[e] = more if totals[e] is None else totals[e] + more
                row = (k - 1) * ghosts + start
                for e in range(comps):
                    halo_mixed[row : row + CHUNK, lane(e)] = totals[e].astype(BF16)
        scale = STEP_SIZE * metric[...]
        arrived = matmul(far[...], halo_mixed[...])
        for e in range(comps):
            states[first + i + 1, e] = base[e] - scale * arrived[:, lane(e)]

    def send_reverse(j):
        for e in range(comps):
            weighted = metric[...] * adjoint[e]
            high = weighted.astype(BF16)
            split[:blocks, lane(e)] = high
            split[blocks:, lane(e)] = (weighted - high.astype(F32)).astype(BF16)
        halo_pulled[...] = matmul(far_t[...], split[...])
        for k in range(1, slots):
            for start in range(0, ghosts, CHUNK):
                row = (k - 1) * ghosts + start
                totals = [None] * comps
                for e in range(comps):
                    term = halo_pulled[row : row + CHUNK, lane(e)]
                    for c in range(comps):
                        more = mixing[k, e, c] * term
                        totals[c] = more if totals[c] is None else totals[c] + more
                for c in range(comps):
                    far_mixed[c * ghosts + start : c * ghosts + start + CHUNK, lane(k - 1)] = totals[
                        c
                    ].astype(BF16)
        right = jnp.concatenate([lift[k] for k in range(1, slots)], axis=0)
        packets = matmul(far_mixed[...], right).astype(BF16)
        for d, offset in enumerate(OFFSETS):
            for c in range(comps):
                row = c * ghosts + d * halo
                rev_out[j, d, :, lane(c)] = packets[row : row + halo]

            @pl.when(exists(p - offset))
            def _():
                rev_copy(j, d, p - offset).start()

    def reverse_sum(n):
        by_cosine = jnp.zeros((8, nodes), F32)
        by_sine = jnp.zeros((8, nodes), F32)
        for e in range(comps):
            value = adjoint[e]
            by_cosine += jnp.sum((value * sources[1, e]).reshape(blocks // 8, 8, nodes), axis=0)
            by_sine += jnp.sum((value * sources[0, e]).reshape(blocks // 8, 8, nodes), axis=0)
        both = cosines[pl.ds(n, 1), :] * by_cosine - sines[pl.ds(n, 1), :] * by_sine
        partial[pl.ds(n, 1), :] = jnp.sum(both, axis=0, keepdims=True)

    def reverse_near(n):
        pulled[...] = matmul(near_t[...], split[...])
        for k in range(slots):
            for start in range(0, blocks, CHUNK):
                some = slice(start, start + CHUNK)
                totals = [None] * comps
                for e in range(comps):
                    if k == 0:
                        term = metric[some, :] * adjoint[e, some, :]
                    else:
                        row = (k - 1) * blocks + start
                        term = pulled[row : row + CHUNK, lane(e)]
                    for c in range(comps):
                        more = mixing[k, e, c] * term
                        totals[c] = more if totals[c] is None else totals[c] + more
                for c in range(comps):
                    mixed[c * blocks + start : c * blocks + start + CHUNK, lane(k)] = totals[c].astype(
                        BF16
                    )
        right = jnp.concatenate([lift[k] for k in range(slots)], axis=0)
        pushed = matmul(mixed[...], right)
        inner = jnp.where(n > 0, 1.0, 0.0).astype(F32)
        for c in range(comps):
            state = states[n, c]
            bent = jnp.tanh(state)
            fall = STEP_SIZE * (1.0 - bent * bent)
            slope[c] = fall
            grown = adjoint[c] + inner * (weight[c] * state)
            base[c] = grown - fall * pushed[c * blocks : (c + 1) * blocks]

    def reverse_far(j):
        for d, offset in enumerate(OFFSETS):

            @pl.when(exists(p + offset))
            def _():
                rev_copy(j, d, p).wait_recv()

        ghost = jnp.concatenate([rev_in[j, d] for d in range(4)], axis=0)
        arrived = matmul(pick_t[...], ghost)
        for c in range(comps):
            adjoint[c] = base[c] - slope[c] * arrived[:, lane(c)]

    loads[0].wait()
    squash(lambda c: states[first, c])
    near_peers = sum(exists(p + offset).astype(jnp.int32) for offset in OFFSETS)
    far_peers = t * (plane - 1 + 2 * (layers - 1))
    pl.semaphore_wait(barrier, near_peers + 1 + far_peers)
    send_forward(0)

    @pl.when(t == 0)
    def _():
        state_copy(0).start()

    loads[1].wait()
    for k in range(slots):
        lift_t[:, lane(k)] = lift[k].astype(F32).T.astype(BF16)
    pick_t[...] = pick[...].T.astype(BF16)
    row_of = lax.broadcasted_iota(jnp.int32, (levels, nodes), 0)
    angles = jnp.zeros((levels, nodes), F32)
    for n in range(levels):
        angles = jnp.where(row_of == n, pitch[n], angles)
    cosines[...] = jnp.cos(angles)
    sines[...] = jnp.sin(angles)
    column = lax.broadcasted_iota(jnp.int32, (blocks, blocks), 1)
    for k in range(1, slots):
        wanted = faces[:, k - 1 : k]
        chosen = jnp.where(wanted == column, 1.0, 0.0)
        near[(k - 1) * blocks : k * blocks, :] = chosen.astype(BF16)
        turned = chosen.T.astype(BF16)
        near_t[(k - 1) * blocks : k * blocks, :blocks] = turned
        near_t[(k - 1) * blocks : k * blocks, blocks:] = turned
    slot_of = lax.rem(column, ghosts)
    for pair in range(2):
        left = faces[:, 2 * pair : 2 * pair + 1] - blocks
        right = faces[:, 2 * pair + 1 : 2 * pair + 2] - blocks
        wanted = jnp.where(column < ghosts, left, right)
        chosen = jnp.where(wanted == slot_of, 1.0, 0.0)
        far[:, pair * blocks : (pair + 1) * blocks] = chosen.astype(BF16)
        turned = chosen.T.astype(BF16)
        far_t[pair * blocks : (pair + 1) * blocks, :blocks] = turned
        far_t[pair * blocks : (pair + 1) * blocks, blocks:] = turned
    loads[2].wait()
    loads[3].wait()
    last = half - 2 + t

    def forward_level(i, carry):
        forward_near(i)
        forward_far(i)

        @pl.when(i < last)
        def _():
            squash(lambda c: states[first + i + 1, c])
            send_forward(i + 1)

        @pl.when(t == 0)
        def _():
            state_copy(i + 1).start()

        return carry

    lax.fori_loop(0, half - 1 + t, forward_level, 0)

    for load in loads[4:]:
        load.wait()

    @pl.when(t == 1)
    def _():
        for e in range(comps):
            adjoint[e] = adjoint[e] + weight[e] * states[levels, e]

        def reverse_level(j, carry):
            n = levels - 1 - j

            @pl.when(n < half)
            def _():
                state_copy(n).wait_recv()

            send_reverse(j)
            reverse_sum(n)
            reverse_near(n)
            reverse_far(j)

            @pl.when(n == half)
            def _():
                kept[...] = adjoint[...]
                keep_copy.start()

            return carry

        lax.fori_loop(0, levels - 1, reverse_level, 0)
        state_copy(0).wait_recv()
        reverse_sum(0)
        plane_parts[spot] = partial[...]
        for r in range(1, plane):
            plane_copy(r).start()
        send_reverse(levels - 1)
        reverse_near(0)
        reverse_far(levels - 1)
        end_copy.start()
        for r in range(1, plane):
            other = lax.rem(spot + r, plane)
            pltpu.make_async_remote_copy(
                src_ref=partial,
                dst_ref=plane_parts.at[other],
                send_sem=plane_send.at[r],
                recv_sem=plane_recv.at[other],
                device_id=(1, p),
                device_id_type=MESH,
            ).wait_recv()
        total = plane_parts[0]
        for s in range(1, plane):
            total = total + plane_parts[s]
        plane_sum[...] = total
        layer_parts[layer] = total
        for r in range(layers):
            layer_copy(r, 0).start()
            if r > 0:
                layer_copy(r, 1).start()

    def layer_wait(r):
        other = lax.rem(layer + r, layers)
        pltpu.make_async_remote_copy(
            src_ref=plane_sum,
            dst_ref=layer_parts.at[other],
            send_sem=layer_send.at[0, r],
            recv_sem=layer_recv.at[other],
            device_id=(1 - t, p),
            device_id_type=MESH,
        ).wait_recv()

    for r in range(1, layers):
        layer_wait(r)

    @pl.when(t == 0)
    def _():
        layer_wait(0)

    total = layer_parts[0]
    for s in range(1, layers):
        total = total + layer_parts[s]
    norm = math.sqrt(comps * nodes * blocks * n_space)
    for n in range(levels):
        grads[n] = STEP_SIZE * jnp.sum(total[n : n + 1, :]) / norm

    def drain(i, carry):
        for d, offset in enumerate(OFFSETS):

            @pl.when(exists(p + offset))
            def _():
                fwd_copy(i, d, p).wait_send()

        return carry

    lax.fori_loop(0, half - 1 + t, drain, 0)

    @pl.when(t == 0)
    def _():
        end_copy.wait_recv()
        for i in range(half):
            state_copy(i).wait_send()

    @pl.when(t == 1)
    def _():
        def drain_reverse(j, carry):
            for d, offset in enumerate(OFFSETS):

                @pl.when(exists(p - offset))
                def _():
                    rev_copy(j, d, p).wait_send()

            return carry

        lax.fori_loop(0, levels, drain_reverse, 0)
        keep_copy.wait()
        end_copy.wait_send()
        for r in range(1, plane):
            plane_copy(r).wait_send()
        for r in range(layers):
            layer_copy(r, 0).wait_send()
            if r > 0:
                layer_copy(r, 1).wait_send()


def solution(mesh):
    n_space = mesh.shape["space"]
    plane = 16 if n_space % 16 == 0 else 4

    def shards(
        checkpoints, sources, pitch, metric, obj_weight, adjoint_end, lift, mixing, faces, send_idx
    ):
        comps, blocks, nodes = obj_weight.shape
        slots = lift.shape[0]
        levels = pitch.shape[0]
        half = levels // 2
        halo = send_idx.shape[2]
        ghosts = 4 * halo
        wide = comps * nodes
        links = slots - 1
        layers = n_space // plane
        vmem = pltpu.VMEM
        dma = pltpu.SemaphoreType.DMA
        field = (comps, blocks, nodes)
        scratch = [
            vmem((levels + 1, *field), F32),
            vmem((2, *field), F32),
            vmem((blocks, nodes), F32),
            vmem(field, F32),
            vmem(field, F32),
            vmem(field, F32),
            vmem((slots, nodes, nodes), BF16),
            vmem((nodes, slots * nodes), BF16),
            vmem((levels, nodes), F32),
            vmem((levels, nodes), F32),
            vmem((ghosts, blocks), F32),
            vmem((blocks, ghosts), BF16),
            vmem((links * blocks, blocks), BF16),
            vmem((links * blocks, 2 * blocks), BF16),
            vmem((blocks, links * ghosts), BF16),
            vmem((links * ghosts, 2 * blocks), BF16),
            vmem((blocks, wide), BF16),
            vmem((links * blocks, wide), BF16),
            vmem((slots, comps * blocks, nodes), F32),
            vmem(field, F32),
            vmem(field, F32),
            vmem((comps * ghosts, links * nodes), F32),
            vmem((links * ghosts, wide), BF16),
            vmem((2 * blocks, wide), BF16),
            vmem((links * blocks, wide), F32),
            vmem((links * ghosts, wide), F32),
            vmem((comps * blocks, slots * nodes), BF16),
            vmem((comps * ghosts, links * nodes), BF16),
            vmem((half, 4, halo, wide), BF16),
            vmem((half, 4, halo, wide), BF16),
            vmem((levels, 4, halo, wide), BF16),
            vmem((levels, 4, halo, wide), BF16),
            vmem((levels, nodes), F32),
            vmem((plane, levels, nodes), F32),
            vmem((levels, nodes), F32),
            vmem((layers, levels, nodes), F32),
            dma((6,)),
            dma((half, 4)),
            dma((half, 4)),
            dma((levels, 4)),
            dma((levels, 4)),
            dma((half,)),
            dma((half,)),
            dma((plane,)),
            dma((plane,)),
            dma((2, layers)),
            dma((layers,)),
            dma((2,)),
            dma,
        ]
        anywhere = pl.BlockSpec(memory_space=pl.ANY)
        scalars = pl.BlockSpec(memory_space=pltpu.SMEM)
        return pl.pallas_call(
            functools.partial(sweep, n_space, plane),
            out_shape=(
                jax.ShapeDtypeStruct((1, *field), F32),
                jax.ShapeDtypeStruct((levels,), F32),
            ),
            in_specs=[
                anywhere,
                anywhere,
                scalars,
                anywhere,
                anywhere,
                anywhere,
                anywhere,
                scalars,
                pl.BlockSpec(memory_space=pltpu.VMEM),
                scalars,
            ],
            out_specs=(anywhere, scalars),
            scratch_shapes=scratch,
            compiler_params=pltpu.CompilerParams(
                collective_id=0, has_side_effects=True, vmem_limit_bytes=48 * 1024 * 1024
            ),
            name="adjoint_window",
        )(checkpoints, sources, pitch, metric, obj_weight, adjoint_end, lift, mixing, faces, send_idx)

    return jax.shard_map(
        shards,
        mesh=mesh,
        in_specs=(
            P("tm", None, "space", None),
            P(None, None, "space", None),
            P(),
            P("space", None),
            P(None, "space", None),
            P(None, "space", None),
            P(),
            P(),
            P("space", None),
            P("space", None, None),
        ),
        out_specs=(P("tm", None, "space", None), P()),
        check_vma=False,
    )
```

profile of v0, /device:TPU:1, one launch (start us, length us, event | category | flops | bytes accessed | tf_op | source)
XLA Modules:
  0.0 97.4 jit_solution(9785507376150852552)
XLA Ops:
  0.6 0.0 copy-start.7
  0.6 0.0 copy-start.5
  0.7 0.8 copy.12.faces
  1.5 0.0 copy-done.7
  1.5 0.0 copy-done.5
  1.5 0.0 copy-start
  1.5 1.1 %copy-done = f32[2,5,128,128]{3,2,1,0:T(8,128)S(1)} copy-done((f32[2,5,128,128]{3,2,1,0:T(8,128)S(1)}, f32[2,5,128,128]{3,2,1,0:T(8,128)}, u32[]{:S(2)}) %copy-start) | copy-done | bytes 655384
  2.6 0.0 copy-start.1
  2.6 1.0 copy-done.1
  3.5 0.0 copy-start.2
  3.6 1.0 copy-done.2
  4.5 0.0 copy-start.3
  4.5 1.0 copy-done.3
  5.5 0.0 copy-start.4
  5.5 0.9 copy-done.4
  6.4 0.0 copy-start.6
  6.4 0.7 copy-done.6
  7.1 0.0 copy-start.8
  7.1 0.7 copy-done.8
  7.8 88.3 %adjoint_window.1 = (f32[1,5,128,128]{3,2,1,0:T(8,128)S(1)}, f32[8]{0:T(128)S(1)}) custom-call(f32[1,5,128,128]{3,2,1,0:T(8,128)S(1)} %copy-done.1, f32[2,5,128,128]{3,2,1,0:T(8,128)S(1)} %copy-done, f32[8]{0:T(128)S(1)} %copy-done.8, f32[128,128]{1,0:T(8,128)S(1)} %copy-done.5, f32[5,128,128]{2,1,0:T(8,128)S(1)} %copy-done.2, f32[5,128,128]{2,1,0:T(8,128)S(1)} %copy-done.3, ...), custom_call_target="tpu_custom_call" | custom-call | tf_op jit(solution)/shard_map/adjoint_window/pallas_call | solution.py:612
  96.1 0.7 copy.15
  96.9 0.5 copy.16
Async XLA Ops:
  0.6 0.8 copy-start.7
  0.6 0.8 copy-start.5
  1.5 1.1 %copy-start = (f32[2,5,128,128]{3,2,1,0:T(8,128)S(1)}, f32[2,5,128,128]{3,2,1,0:T(8,128)}, u32[]{:S(2)}) copy-start(f32[2,5,128,128]{3,2,1,0:T(8,128)} %sources_in.1) | copy-start | bytes 1966084
  2.6 1.0 copy-start.1
  3.5 1.0 copy-start.2
  4.5 1.0 copy-start.3
  5.5 0.9 copy-start.4
  6.4 0.7 copy-start.6
  7.1 0.7 copy-start.8
where the time goes:
time: 97.7 us; the launch traced here: 97.4 us
  Pallas kernels  88.3 us (90%)
  local copies, waits for them, and re-layouts  8.37 us (9%)
    pallas_call x1, Pallas kernels, shards(): pl.pallas_call(functools.partial(sweep, n_space, plane), out_shape=(jax.S...  88.3 us
    unnamed x21, local copies, waits for them, and re-layouts  8.37 us

commit v1 on v0

--- a/solution.py
+++ b/solution.py
@@ -9,6 +9,7 @@
 from jax.sharding import PartitionSpec as P
 
 OFFSETS = (1, -1, 2, -2)
+FARTHEST_FIRST = (2, 3, 0, 1)
 STEP_SIZE = 0.5
 MESH = pl.DeviceIdType.MESH
 F32, BF16 = jnp.float32, jnp.bfloat16
@@ -218,12 +219,12 @@
 
     def send_forward(i):
         packets = matmul(pick[...].astype(BF16), squashed[...]).astype(BF16)
-        for d, offset in enumerate(OFFSETS):
+        for d in FARTHEST_FIRST:
             fwd_out[i, d] = packets[d * halo : (d + 1) * halo]
 
-            @pl.when(exists(p + offset))
+            @pl.when(exists(p + OFFSETS[d]))
             def _():
-                fwd_copy(i, d, p + offset).start()
+                fwd_copy(i, d, p + OFFSETS[d]).start()
 
     def forward_near(i):
         gathered[...] = matmul(near[...], squashed[...]).astype(BF16)
@@ -295,14 +296,14 @@
                     ].astype(BF16)
         right = jnp.concatenate([lift[k] for k in range(1, slots)], axis=0)
         packets = matmul(far_mixed[...], right).astype(BF16)
-        for d, offset in enumerate(OFFSETS):
+        for d in FARTHEST_FIRST:
             for c in range(comps):
                 row = c * ghosts + d * halo
                 rev_out[j, d, :, lane(c)] = packets[row : row + halo]
 
-            @pl.when(exists(p - offset))
+            @pl.when(exists(p - OFFSETS[d]))
             def _():
-                rev_copy(j, d, p - offset).start()
+                rev_copy(j, d, p - OFFSETS[d]).start()
 
     def reverse_sum(n):
         by_cosine = jnp.zeros((8, nodes), F32)
@@ -377,22 +378,21 @@
         angles = jnp.where(row_of == n, pitch[n], angles)
     cosines[...] = jnp.cos(angles)
     sines[...] = jnp.sin(angles)
-    column = lax.broadcasted_iota(jnp.int32, (blocks, blocks), 1)
+    row_at = lax.broadcasted_iota(jnp.int32, (blocks, blocks), 0)
     for k in range(1, slots):
-        wanted = faces[:, k - 1 : k]
-        chosen = jnp.where(wanted == column, 1.0, 0.0)
-        near[(k - 1) * blocks : k * blocks, :] = chosen.astype(BF16)
-        turned = chosen.T.astype(BF16)
+        chosen = jnp.where(faces[k - 1 : k, :] == row_at, 1.0, 0.0)
+        near[(k - 1) * blocks : k * blocks, :] = chosen.T.astype(BF16)
+        turned = chosen.astype(BF16)
         near_t[(k - 1) * blocks : k * blocks, :blocks] = turned
         near_t[(k - 1) * blocks : k * blocks, blocks:] = turned
-    slot_of = lax.rem(column, ghosts)
+    slot_at = lax.rem(row_at, ghosts)
     for pair in range(2):
-        left = faces[:, 2 * pair : 2 * pair + 1] - blocks
-        right = faces[:, 2 * pair + 1 : 2 * pair + 2] - blocks
-        wanted = jnp.where(column < ghosts, left, right)
-        chosen = jnp.where(wanted == slot_of, 1.0, 0.0)
-        far[:, pair * blocks : (pair + 1) * blocks] = chosen.astype(BF16)
-        turned = chosen.T.astype(BF16)
+        upper = faces[2 * pair : 2 * pair + 1, :] - blocks
+        lower = faces[2 * pair + 1 : 2 * pair + 2, :] - blocks
+        wanted = jnp.where(row_at < ghosts, upper, lower)
+        chosen = jnp.where(wanted == slot_at, 1.0, 0.0)
+        far[:, pair * blocks : (pair + 1) * blocks] = chosen.T.astype(BF16)
+        turned = chosen.astype(BF16)
         far_t[pair * blocks : (pair + 1) * blocks, :blocks] = turned
         far_t[pair * blocks : (pair + 1) * blocks, blocks:] = turned
     loads[2].wait()
@@ -630,10 +630,10 @@
             out_specs=(anywhere, scalars),
             scratch_shapes=scratch,
             compiler_params=pltpu.CompilerParams(
-                collective_id=0, has_side_effects=True, vmem_limit_bytes=48 * 1024 * 1024
+                collective_id=0, has_side_effects=True, vmem_limit_bytes=67043328
             ),
             name="adjoint_window",
-        )(checkpoints, sources, pitch, metric, obj_weight, adjoint_end, lift, mixing, faces, send_idx)
+        )(checkpoints, sources, pitch, metric, obj_weight, adjoint_end, lift, mixing, faces.T, send_idx)
 
     return jax.shard_map(
         shards,

time: 97.7 us -> 91.1 us (0.932)
  local copies, waits for them, and re-layouts: 8.37 us -> 2.23 us
    unnamed x21 -> x4, local copies, waits for them, and re-layouts: 8.37 us -> 2.23 us
where the time goes in v1:
time: 91.1 us; the launch traced here: 90.9 us
  Pallas kernels  88 us (97%)
  local copies, waits for them, and re-layouts  2.23 us (2%)
    pallas_call x1, Pallas kernels, shards(): pl.pallas_call(functools.partial(sweep, n_space, plane), out_shape=(jax.S...  88 us
    unnamed x4, local copies, waits for them, and re-layouts  2.23 us

profile of v1, /device:TPU:1, one launch (start us, length us, event | category | flops | bytes accessed | tf_op | source)
XLA Modules:
  0.0 90.9 jit_solution(17736029397861931824)
XLA Ops:
  0.6 88.0 %adjoint_window.1 = (f32[1,5,128,128]{3,2,1,0:T(8,128)}, f32[8]{0:T(128)}) custom-call(f32[1,5,128,128]{3,2,1,0:T(8,128)} %checkpoint_in.1, f32[2,5,128,128]{3,2,1,0:T(8,128)} %sources_in.1, f32[8]{0:T(128)} %pitch.1, f32[128,128]{1,0:T(8,128)} %metric_in.1, f32[5,128,128]{2,1,0:T(8,128)} %weight_in.1, f32[5,128,128]{2,1,0:T(8,128)} %end_in.1, ...), custom_call_target="tpu_custom_call" | custom-call | tf_op jit(solution)/shard_map/adjoint_window/pallas_call | solution.py:612
  88.6 0.0 copy-start
  88.7 1.7 %copy.14 = f32[1,5,128,128]{3,2,1,0:T(8,128)} copy(f32[1,5,128,128]{3,2,1,0:T(8,128)} %get-tuple-element.4) | data formatting | bytes 655360
  90.4 0.0 copy-done
  90.4 0.5 copy.15
Async XLA Ops:
  88.6 1.7 %copy-start = (f32[8]{0:T(128)S(1)}, f32[8]{0:T(128)}, u32[]{:S(2)}) copy-start(f32[8]{0:T(128)} %get-tuple-element.5) | copy-start | bytes 100

commit v2 on v1

--- a/solution.py
+++ b/solution.py
@@ -67,6 +67,9 @@
     fwd_in,
     rev_out,
     rev_in,
+    bend_out,
+    bend_in,
+    bend_there,
     partial,
     plane_parts,
     plane_sum,
@@ -76,6 +79,9 @@
     fwd_recv,
     rev_send,
     rev_recv,
+    bend_send,
+    bend_recv,
+    bend_sem,
     state_send,
     state_recv,
     plane_send,
@@ -127,6 +133,7 @@
             greet((t, p + offset))
 
     greet((1 - t, p))
+
     for r in range(1, layers):
         greet((1, lax.rem(layer + r, layers) * plane + spot))
 
@@ -145,6 +152,7 @@
 
         @pl.when(jnp.logical_not(exists(p - offset)))
         def _():
+            bend_in[d] = jnp.zeros(bend_in.shape[1:], BF16)
             for i in range(half):
                 fwd_in[i, d] = jnp.zeros(fwd_in.shape[2:], BF16)
 
@@ -173,6 +181,16 @@
             device_id_type=MESH,
         )
 
+    def bend_copy(d, device):
+        return pltpu.make_async_remote_copy(
+            src_ref=bend_out.at[d],
+            dst_ref=bend_in.at[d],
+            send_sem=bend_send.at[d],
+            recv_sem=bend_recv.at[d],
+            device_id=(t, device),
+            device_id_type=MESH,
+        )
+
     def state_copy(i):
         return pltpu.make_async_remote_copy(
             src_ref=states.at[i],
@@ -203,6 +221,14 @@
             device_id_type=MESH,
         )
 
+    bend_pass = pltpu.make_async_remote_copy(
+        src_ref=bend_in,
+        dst_ref=bend_there,
+        send_sem=bend_sem.at[0],
+        recv_sem=bend_sem.at[1],
+        device_id=(1 - t, p),
+        device_id_type=MESH,
+    )
     end_copy = pltpu.make_async_remote_copy(
         src_ref=adjoint,
         dst_ref=bounds.at[0],
@@ -305,11 +331,11 @@
             def _():
                 rev_copy(j, d, p - OFFSETS[d]).start()
 
-    def reverse_sum(n):
+    def reverse_sum(n, field):
         by_cosine = jnp.zeros((8, nodes), F32)
         by_sine = jnp.zeros((8, nodes), F32)
         for e in range(comps):
-            value = adjoint[e]
+            value = field[e]
             by_cosine += jnp.sum((value * sources[1, e]).reshape(blocks // 8, 8, nodes), axis=0)
             by_sine += jnp.sum((value * sources[0, e]).reshape(blocks // 8, 8, nodes), axis=0)
         both = cosines[pl.ds(n, 1), :] * by_cosine - sines[pl.ds(n, 1), :] * by_sine
@@ -356,6 +382,37 @@
         arrived = matmul(pick_t[...], ghost)
         for c in range(comps):
             adjoint[c] = base[c] - slope[c] * arrived[:, lane(c)]
+
+    def send_bend():
+        for e in range(comps):
+            bent = jnp.tanh(states[1, e])
+            turning = cosines[0:1, :] * sources[1, e] - sines[0:1, :] * sources[0, e]
+            squashed[:, lane(e)] = (STEP_SIZE * (1.0 - bent * bent) * turning).astype(BF16)
+        packets = matmul(pick[...].astype(BF16), squashed[...]).astype(BF16)
+        for d, offset in enumerate(OFFSETS):
+            bend_out[d] = packets[d * halo : (d + 1) * halo]
+
+            @pl.when(exists(p + offset))
+            def _():
+                bend_copy(d, p + offset).start()
+
+        for d, offset in enumerate(OFFSETS):
+
+            @pl.when(exists(p - offset))
+            def _():
+                bend_copy(d, p).wait_recv()
+
+        bend_pass.start()
+
+    def last_sum(j):
+        reverse_sum(0, base)
+        bend_pass.wait_recv()
+        sent = jnp.zeros((halo, nodes), F32)
+        for d in range(4):
+            both = rev_out[j, d].astype(F32) * bend_there[d].astype(F32)
+            for c in range(comps):
+                sent += both[:, lane(c)]
+        partial[0:1, :] = partial[0:1, :] - jnp.sum(sent, axis=0, keepdims=True)
 
     loads[0].wait()
     squash(lambda c: states[first, c])
@@ -419,6 +476,10 @@
     for load in loads[4:]:
         load.wait()
 
+    @pl.when(t == 0)
+    def _():
+        send_bend()
+
     @pl.when(t == 1)
     def _():
         for e in range(comps):
@@ -432,8 +493,9 @@
                 state_copy(n).wait_recv()
 
             send_reverse(j)
-            reverse_sum(n)
+            reverse_sum(n, adjoint)
             reverse_near(n)
+
             reverse_far(j)
 
             @pl.when(n == half)
@@ -443,16 +505,19 @@
 
             return carry
 
-        lax.fori_loop(0, levels - 1, reverse_level, 0)
-        state_copy(0).wait_recv()
-        reverse_sum(0)
+        lax.fori_loop(0, levels - 2, reverse_level, 0)
+        state_copy(1).wait_recv()
+        send_reverse(levels - 2)
+        reverse_sum(1, adjoint)
+        reverse_near(1)
+        last_sum(levels - 2)
         plane_parts[spot] = partial[...]
         for r in range(1, plane):
             plane_copy(r).start()
+        reverse_far(levels - 2)
+        state_copy(0).wait_recv()
         send_reverse(levels - 1)
         reverse_near(0)
-        reverse_far(levels - 1)
-        end_copy.start()
         for r in range(1, plane):
             other = lax.rem(spot + r, plane)
             pltpu.make_async_remote_copy(
@@ -472,6 +537,8 @@
             layer_copy(r, 0).start()
             if r > 0:
                 layer_copy(r, 1).start()
+        reverse_far(levels - 1)
+        end_copy.start()
 
     def layer_wait(r):
         other = lax.rem(layer + r, layers)
@@ -514,6 +581,13 @@
         end_copy.wait_recv()
         for i in range(half):
             state_copy(i).wait_send()
+        for d, offset in enumerate(OFFSETS):
+
+            @pl.when(exists(p + offset))
+            def _():
+                bend_copy(d, p).wait_send()
+
+        bend_pass.wait_send()
 
     @pl.when(t == 1)
     def _():
@@ -589,6 +663,9 @@
             vmem((half, 4, halo, wide), BF16),
             vmem((levels, 4, halo, wide), BF16),
             vmem((levels, 4, halo, wide), BF16),
+            vmem((4, halo, wide), BF16),
+            vmem((4, halo, wide), BF16),
+            vmem((4, halo, wide), BF16),
             vmem((levels, nodes), F32),
             vmem((plane, levels, nodes), F32),
             vmem((levels, nodes), F32),
@@ -598,6 +675,9 @@
             dma((half, 4)),
             dma((levels, 4)),
             dma((levels, 4)),
+            dma((4,)),
+            dma((4,)),
+            dma((2,)),
             dma((half,)),
             dma((half,)),
             dma((plane,)),

time: 91.1 us -> 87.5 us (0.960)
  Pallas kernels: 88 us -> 84.4 us
    pallas_call x1, Pallas kernels: 88 us -> 84.4 us  [shards(): pl.pallas_call(functools.partial(sweep, n_space, plane), out_shape=(jax.S...]
where the time goes in v2:
time: 87.5 us; the launch traced here: 87.3 us
  Pallas kernels  84.4 us (96%)
  local copies, waits for them, and re-layouts  2.23 us (3%)
    pallas_call x1, Pallas kernels, shards(): pl.pallas_call(functools.partial(sweep, n_space, plane), out_shape=(jax.S...  84.4 us
    unnamed x4, local copies, waits for them, and re-layouts  2.23 us

profile of v2, /device:TPU:1, one launch (start us, length us, event | category | flops | bytes accessed | tf_op | source)
XLA Modules:
  0.0 87.3 jit_solution(7748856524931271379)
XLA Ops:
  0.6 84.4 %adjoint_window.1 = (f32[1,5,128,128]{3,2,1,0:T(8,128)}, f32[8]{0:T(128)}) custom-call(f32[1,5,128,128]{3,2,1,0:T(8,128)} %checkpoint_in.1, f32[2,5,128,128]{3,2,1,0:T(8,128)} %sources_in.1, f32[8]{0:T(128)} %pitch.1, f32[128,128]{1,0:T(8,128)} %metric_in.1, f32[5,128,128]{2,1,0:T(8,128)} %weight_in.1, f32[5,128,128]{2,1,0:T(8,128)} %end_in.1, ...), custom_call_target="tpu_custom_call" | custom-call | tf_op jit(solution)/shard_map/adjoint_window/pallas_call | solution.py:692
  85.0 0.0 copy-start
  85.0 1.7 %copy.14 = f32[1,5,128,128]{3,2,1,0:T(8,128)} copy(f32[1,5,128,128]{3,2,1,0:T(8,128)} %get-tuple-element.4) | data formatting | bytes 655360
  86.7 0.0 copy-done
  86.8 0.5 copy.15
Async XLA Ops:
  85.0 1.7 %copy-start = (f32[8]{0:T(128)S(1)}, f32[8]{0:T(128)}, u32[]{:S(2)}) copy-start(f32[8]{0:T(128)} %get-tuple-element.5) | copy-start | bytes 100

commit v3 on v2

--- a/solution.py
+++ b/solution.py
@@ -90,6 +90,7 @@
     layer_recv,
     end_sem,
     out_sem,
+    hello,
 ):
     comps, blocks, nodes = states.shape[1:]
     slots = lift.shape[0]
@@ -134,13 +135,19 @@
 
     greet((1 - t, p))
 
-    for r in range(1, layers):
-        greet((1, lax.rem(layer + r, layers) * plane + spot))
+    def in_layer(r):
+        return (1, lax.rem(layer + r + layers, layers) * plane + spot)
 
     @pl.when(t == 1)
     def _():
-        for r in range(1, plane):
-            greet((1, layer * plane + lax.rem(spot + r, plane)))
+        greet(in_layer(1))
+        greet(in_layer(-1))
+
+    def call(which, distance):
+        for r in (distance, -distance):
+            pl.semaphore_signal(
+                hello.at[which], inc=1, device_id=in_layer(r), device_id_type=MESH
+            )
 
     lane_of = lax.broadcasted_iota(jnp.int32, (1, blocks), 1)
     for d in range(4):
@@ -417,13 +424,16 @@
     loads[0].wait()
     squash(lambda c: states[first, c])
     near_peers = sum(exists(p + offset).astype(jnp.int32) for offset in OFFSETS)
-    far_peers = t * (plane - 1 + 2 * (layers - 1))
-    pl.semaphore_wait(barrier, near_peers + 1 + far_peers)
+    pl.semaphore_wait(barrier, near_peers + 1 + 2 * t)
     send_forward(0)
 
     @pl.when(t == 0)
     def _():
         state_copy(0).start()
+
+    @pl.when(t == 1)
+    def _():
+        call(0, 1)
 
     loads[1].wait()
     for k in range(slots):
@@ -482,6 +492,8 @@
 
     @pl.when(t == 1)
     def _():
+        pl.semaphore_wait(hello.at[0], 2)
+        call(1, 2)
         for e in range(comps):
             adjoint[e] = adjoint[e] + weight[e] * states[levels, e]
 
@@ -510,6 +522,8 @@
         send_reverse(levels - 2)
         reverse_sum(1, adjoint)
         reverse_near(1)
+        pl.semaphore_wait(hello.at[1], 2)
+        call(2, 2)
         last_sum(levels - 2)
         plane_parts[spot] = partial[...]
         for r in range(1, plane):
@@ -518,6 +532,7 @@
         state_copy(0).wait_recv()
         send_reverse(levels - 1)
         reverse_near(0)
+        pl.semaphore_wait(hello.at[2], 2)
         for r in range(1, plane):
             other = lax.rem(spot + r, plane)
             pltpu.make_async_remote_copy(
@@ -686,6 +701,7 @@
             dma((layers,)),
             dma((2,)),
             dma,
+            pltpu.SemaphoreType.REGULAR((3,)),
         ]
         anywhere = pl.BlockSpec(memory_space=pl.ANY)
         scalars = pl.BlockSpec(memory_space=pltpu.SMEM)

time: 87.5 us -> 85.9 us (0.982)
  Pallas kernels: 84.4 us -> 82.8 us
    pallas_call x1, Pallas kernels: 84.4 us -> 82.8 us  [shards(): pl.pallas_call(functools.partial(sweep, n_space, plane), out_shape=(jax.S...]
where the time goes in v3:
time: 85.9 us; the launch traced here: 85.7 us
  Pallas kernels  82.8 us (96%)
  local copies, waits for them, and re-layouts  2.23 us (3%)
    pallas_call x1, Pallas kernels, shards(): pl.pallas_call(functools.partial(sweep, n_space, plane), out_shape=(jax.S...  82.8 us
    unnamed x4, local copies, waits for them, and re-layouts  2.23 us

profile of v3, /device:TPU:1, one launch (start us, length us, event | category | flops | bytes accessed | tf_op | source)
XLA Modules:
  0.0 85.7 jit_solution(13242216932218101059)
XLA Ops:
  0.6 82.8 %adjoint_window.1 = (f32[1,5,128,128]{3,2,1,0:T(8,128)}, f32[8]{0:T(128)}) custom-call(f32[1,5,128,128]{3,2,1,0:T(8,128)} %checkpoint_in.1, f32[2,5,128,128]{3,2,1,0:T(8,128)} %sources_in.1, f32[8]{0:T(128)} %pitch.1, f32[128,128]{1,0:T(8,128)} %metric_in.1, f32[5,128,128]{2,1,0:T(8,128)} %weight_in.1, f32[5,128,128]{2,1,0:T(8,128)} %end_in.1, ...), custom_call_target="tpu_custom_call" | custom-call | tf_op jit(solution)/shard_map/adjoint_window/pallas_call | solution.py:708
  83.4 0.0 copy-start
  83.4 1.7 %copy.14 = f32[1,5,128,128]{3,2,1,0:T(8,128)} copy(f32[1,5,128,128]{3,2,1,0:T(8,128)} %get-tuple-element.4) | data formatting | bytes 655360
  85.2 0.0 copy-done
  85.2 0.5 copy.15
Async XLA Ops:
  83.4 1.7 %copy-start = (f32[8]{0:T(128)S(1)}, f32[8]{0:T(128)}, u32[]{:S(2)}) copy-start(f32[8]{0:T(128)} %get-tuple-element.5) | copy-start | bytes 100

commit v4 on v3

--- a/solution.py
+++ b/solution.py
@@ -51,6 +51,15 @@
     near_t,
     far,
     far_t,
+    far_pick,
+    cross,
+    pick_wide,
+    thirds,
+    picked,
+    picked_scale,
+    gain,
+    back_split,
+    ahead,
     squashed,
     gathered,
     lifted,
@@ -246,6 +255,18 @@
     )
     keep_copy = pltpu.make_async_copy(kept, bounds.at[0], out_sem)
 
+    def in_halves(value, where, columns):
+        rows = value.shape[0]
+        high = value.astype(BF16)
+        where[:rows, columns] = high
+        where[rows:, columns] = (value - high.astype(F32)).astype(BF16)
+
+    def in_thirds(value, columns):
+        for part in range(3):
+            high = value.astype(BF16)
+            thirds[part * blocks : (part + 1) * blocks, columns] = high
+            value = value - high.astype(F32)
+
     def squash(state):
         for c in range(comps):
             squashed[:, lane(c)] = jnp.tanh(state(c)).astype(BF16)
@@ -302,18 +323,34 @@
                 row = (k - 1) * ghosts + start
                 for e in range(comps):
                     halo_mixed[row : row + CHUNK, lane(e)] = totals[e].astype(BF16)
+
+    def forward_ahead():
+        for e in range(comps):
+            in_thirds(base[e], lane(e))
+        picked[...] = matmul(pick_wide[...], thirds[...])
+
+    def send_picked(i):
+        change = matmul(far_pick[...], halo_mixed[...])
+        wide_scale = jnp.concatenate([picked_scale[...]] * comps, axis=1)
+        packets = jnp.tanh(picked[...] - wide_scale * change).astype(BF16)
+        for d in FARTHEST_FIRST:
+            fwd_out[i, d] = packets[d * halo : (d + 1) * halo]
+
+            @pl.when(exists(p + OFFSETS[d]))
+            def _():
+                fwd_copy(i, d, p + OFFSETS[d]).start()
+
+    def forward_end(i):
         scale = STEP_SIZE * metric[...]
         arrived = matmul(far[...], halo_mixed[...])
         for e in range(comps):
             states[first + i + 1, e] = base[e] - scale * arrived[:, lane(e)]
 
-    def send_reverse(j):
+    def split_field(field):
         for e in range(comps):
-            weighted = metric[...] * adjoint[e]
-            high = weighted.astype(BF16)
-            split[:blocks, lane(e)] = high
-            split[blocks:, lane(e)] = (weighted - high.astype(F32)).astype(BF16)
-        halo_pulled[...] = matmul(far_t[...], split[...])
+            in_halves(metric[...] * field[e], split, lane(e))
+
+    def far_product():
         for k in range(1, slots):
             for start in range(0, ghosts, CHUNK):
                 row = (k - 1) * ghosts + start
@@ -328,7 +365,10 @@
                         c
                     ].astype(BF16)
         right = jnp.concatenate([lift[k] for k in range(1, slots)], axis=0)
-        packets = matmul(far_mixed[...], right).astype(BF16)
+        return matmul(far_mixed[...], right)
+
+    def ship_reverse(j, product):
+        packets = product.astype(BF16)
         for d in FARTHEST_FIRST:
             for c in range(comps):
                 row = c * ghosts + d * halo
@@ -337,6 +377,24 @@
             @pl.when(exists(p - OFFSETS[d]))
             def _():
                 rev_copy(j, d, p - OFFSETS[d]).start()
+
+    def send_reverse(j):
+        halo_pulled[...] = matmul(far_t[...], split[...])
+        ship_reverse(j, far_product())
+
+    def reverse_ahead():
+        split_field(slope)
+        gain[...] = matmul(pick_wide[:, : 2 * blocks], split[...])
+        split_field(base)
+        halo_pulled[...] = matmul(far_t[...], split[...])
+        ahead[...] = far_product()
+
+    def send_ahead(j):
+        for c in range(comps):
+            back = jnp.concatenate([rev_in[j - 1, d, :, lane(c)] for d in range(4)], axis=0)
+            in_halves(gain[:, lane(c)] * back.astype(F32), back_split, lane(c))
+        halo_pulled[...] = matmul(cross[...], back_split[...])
+        ship_reverse(j, ahead[...] - far_product())
 
     def reverse_sum(n, field):
         by_cosine = jnp.zeros((8, nodes), F32)
@@ -378,13 +436,14 @@
             grown = adjoint[c] + inner * (weight[c] * state)
             base[c] = grown - fall * pushed[c * blocks : (c + 1) * blocks]
 
+    def reverse_wait(j):
+        for d, offset in enumerate(OFFSETS):
+
+            @pl.when(exists(p + offset))
+            def _():
+                rev_copy(j, d, p).wait_recv()
+
     def reverse_far(j):
-        for d, offset in enumerate(OFFSETS):
-
-            @pl.when(exists(p + offset))
-            def _():
-                rev_copy(j, d, p).wait_recv()
-
         ghost = jnp.concatenate([rev_in[j, d] for d in range(4)], axis=0)
         arrived = matmul(pick_t[...], ghost)
         for c in range(comps):
@@ -462,18 +521,32 @@
         turned = chosen.astype(BF16)
         far_t[pair * blocks : (pair + 1) * blocks, :blocks] = turned
         far_t[pair * blocks : (pair + 1) * blocks, blocks:] = turned
+    wide_pick = pick[...].astype(BF16)
+    for part in range(3):
+        pick_wide[:, part * blocks : (part + 1) * blocks] = wide_pick
+    far_pick[...] = matmul(wide_pick, far[...]).astype(BF16)
+    crossed = matmul(far_t[:, :blocks], pick_t[...]).astype(BF16)
+    cross[...] = jnp.concatenate([crossed, crossed], axis=1)
     loads[2].wait()
+    in_thirds(STEP_SIZE * metric[...], lane(0))
+    picked_scale[...] = matmul(pick_wide[...], thirds[:, lane(0)])
     loads[3].wait()
     last = half - 2 + t
 
     def forward_level(i, carry):
         forward_near(i)
+        forward_ahead()
         forward_far(i)
+
+        @pl.when(i < last)
+        def _():
+            send_picked(i + 1)
+
+        forward_end(i)
 
         @pl.when(i < last)
         def _():
             squash(lambda c: states[first + i + 1, c])
-            send_forward(i + 1)
 
         @pl.when(t == 0)
         def _():
@@ -496,6 +569,8 @@
         call(1, 2)
         for e in range(comps):
             adjoint[e] = adjoint[e] + weight[e] * states[levels, e]
+        split_field(adjoint)
+        send_reverse(0)
 
         def reverse_level(j, carry):
             n = levels - 1 - j
@@ -504,11 +579,13 @@
             def _():
                 state_copy(n).wait_recv()
 
-            send_reverse(j)
             reverse_sum(n, adjoint)
             reverse_near(n)
-
+            reverse_ahead()
+            reverse_wait(j)
+            send_ahead(j + 1)
             reverse_far(j)
+            split_field(adjoint)
 
             @pl.when(n == half)
             def _():
@@ -519,7 +596,6 @@
 
         lax.fori_loop(0, levels - 2, reverse_level, 0)
         state_copy(1).wait_recv()
-        send_reverse(levels - 2)
         reverse_sum(1, adjoint)
         reverse_near(1)
         pl.semaphore_wait(hello.at[1], 2)
@@ -528,9 +604,12 @@
         plane_parts[spot] = partial[...]
         for r in range(1, plane):
             plane_copy(r).start()
+        reverse_ahead()
+        reverse_wait(levels - 2)
+        send_ahead(levels - 1)
         reverse_far(levels - 2)
+        split_field(adjoint)
         state_copy(0).wait_recv()
-        send_reverse(levels - 1)
         reverse_near(0)
         pl.semaphore_wait(hello.at[2], 2)
         for r in range(1, plane):
@@ -552,6 +631,7 @@
             layer_copy(r, 0).start()
             if r > 0:
                 layer_copy(r, 1).start()
+        reverse_wait(levels - 1)
         reverse_far(levels - 1)
         end_copy.start()
 
@@ -662,6 +742,15 @@
             vmem((links * blocks, 2 * blocks), BF16),
             vmem((blocks, links * ghosts), BF16),
             vmem((links * ghosts, 2 * blocks), BF16),
+            vmem((ghosts, links * ghosts), BF16),
+            vmem((links * ghosts, 2 * ghosts), BF16),
+            vmem((ghosts, 3 * blocks), BF16),
+            vmem((3 * blocks, wide), BF16),
+            vmem((ghosts, wide), F32),
+            vmem((ghosts, nodes), F32),
+            vmem((ghosts, wide), F32),
+            vmem((2 * ghosts, wide), BF16),
+            vmem((comps * ghosts, nodes), F32),
             vmem((blocks, wide), BF16),
             vmem((links * blocks, wide), BF16),
             vmem((slots, comps * blocks, nodes), F32),

time: 85.9 us -> 84 us (0.978)
  Pallas kernels: 82.8 us -> 81 us
    pallas_call x1, Pallas kernels: 82.8 us -> 81 us  [shards(): pl.pallas_call(functools.partial(sweep, n_space, plane), out_shape=(jax.S...]
where the time goes in v4:
time: 84 us; the launch traced here: 83.8 us
  Pallas kernels  81 us (96%)
  local copies, waits for them, and re-layouts  2.23 us (3%)
    pallas_call x1, Pallas kernels, shards(): pl.pallas_call(functools.partial(sweep, n_space, plane), out_shape=(jax.S...  81 us
    unnamed x4, local copies, waits for them, and re-layouts  2.23 us

profile of v4, /device:TPU:1, one launch (start us, length us, event | category | flops | bytes accessed | tf_op | source)
XLA Modules:
  0.0 83.8 jit_solution(12993619162847219601)
XLA Ops:
  0.6 81.0 %adjoint_window.1 = (f32[1,5,128,128]{3,2,1,0:T(8,128)}, f32[8]{0:T(128)}) custom-call(f32[1,5,128,128]{3,2,1,0:T(8,128)} %checkpoint_in.1, f32[2,5,128,128]{3,2,1,0:T(8,128)} %sources_in.1, f32[8]{0:T(128)} %pitch.1, f32[128,128]{1,0:T(8,128)} %metric_in.1, f32[5,128,128]{2,1,0:T(8,128)} %weight_in.1, f32[5,128,128]{2,1,0:T(8,128)} %end_in.1, ...), custom_call_target="tpu_custom_call" | custom-call | tf_op jit(solution)/shard_map/adjoint_window/pallas_call | solution.py:797
  81.6 0.0 copy-start
  81.6 1.7 %copy.14 = f32[1,5,128,128]{3,2,1,0:T(8,128)} copy(f32[1,5,128,128]{3,2,1,0:T(8,128)} %get-tuple-element.4) | data formatting | bytes 655360
  83.3 0.0 copy-done
  83.3 0.5 copy.15
Async XLA Ops:
  81.6 1.7 %copy-start = (f32[8]{0:T(128)S(1)}, f32[8]{0:T(128)}, u32[]{:S(2)}) copy-start(f32[8]{0:T(128)} %get-tuple-element.5) | copy-start | bytes 100

commit v5 on v4

--- a/solution.py
+++ b/solution.py
@@ -25,16 +25,21 @@
     plane,
     checkpoint_in,
     sources_in,
-    pitch,
+    pitch_in,
     metric_in,
     weight_in,
     end_in,
     lift_in,
+    mixing_in,
+    faces_in,
+    send_idx_in,
+    bounds,
+    grads,
+    pitch,
     mixing,
     faces,
     send_idx,
-    bounds,
-    grads,
+    grads_row,
     states,
     sources,
     metric,
@@ -120,17 +125,29 @@
     def lane(c):
         return slice(c * nodes, (c + 1) * nodes)
 
-    loads = [
+    (
+        load_first,
+        load_idx,
+        load_mixing,
+        load_faces,
+        load_pitch,
+        load_lift,
+        load_metric,
+        load_sources,
+        load_weight,
+        load_end,
+    ) = loads = [
         pltpu.make_async_copy(checkpoint_in.at[0], states.at[first], in_sem.at[0]),
+        pltpu.make_async_copy(send_idx_in, send_idx, in_sem.at[6]),
+        pltpu.make_async_copy(mixing_in, mixing, in_sem.at[7]),
+        pltpu.make_async_copy(faces_in, faces, in_sem.at[8]),
+        pltpu.make_async_copy(pitch_in, pitch, in_sem.at[9]),
         pltpu.make_async_copy(lift_in, lift, in_sem.at[1]),
         pltpu.make_async_copy(metric_in, metric, in_sem.at[2]),
         pltpu.make_async_copy(sources_in, sources, in_sem.at[3]),
         pltpu.make_async_copy(weight_in, weight, in_sem.at[4]),
         pltpu.make_async_copy(end_in, adjoint, in_sem.at[5]),
     ]
-    for load in loads:
-        load.start()
-
     barrier = pltpu.get_barrier_semaphore()
 
     def greet(device):
@@ -158,6 +175,10 @@
                 hello.at[which], inc=1, device_id=in_layer(r), device_id_type=MESH
             )
 
+    for load in loads:
+        load.start()
+
+    load_idx.wait()
     lane_of = lax.broadcasted_iota(jnp.int32, (1, blocks), 1)
     for d in range(4):
         for s in range(halo):
@@ -253,7 +274,7 @@
         device_id=(1 - t, p),
         device_id_type=MESH,
     )
-    keep_copy = pltpu.make_async_copy(kept, bounds.at[0], out_sem)
+    keep_copy = pltpu.make_async_copy(kept, bounds.at[0], out_sem.at[0])
 
     def in_halves(value, where, columns):
         rows = value.shape[0]
@@ -480,7 +501,7 @@
                 sent += both[:, lane(c)]
         partial[0:1, :] = partial[0:1, :] - jnp.sum(sent, axis=0, keepdims=True)
 
-    loads[0].wait()
+    load_first.wait()
     squash(lambda c: states[first, c])
     near_peers = sum(exists(p + offset).astype(jnp.int32) for offset in OFFSETS)
     pl.semaphore_wait(barrier, near_peers + 1 + 2 * t)
@@ -494,10 +515,13 @@
     def _():
         call(0, 1)
 
-    loads[1].wait()
+    load_lift.wait()
     for k in range(slots):
         lift_t[:, lane(k)] = lift[k].astype(F32).T.astype(BF16)
     pick_t[...] = pick[...].T.astype(BF16)
+    load_pitch.wait()
+    load_faces.wait()
+    load_mixing.wait()
     row_of = lax.broadcasted_iota(jnp.int32, (levels, nodes), 0)
     angles = jnp.zeros((levels, nodes), F32)
     for n in range(levels):
@@ -527,10 +551,10 @@
     far_pick[...] = matmul(wide_pick, far[...]).astype(BF16)
     crossed = matmul(far_t[:, :blocks], pick_t[...]).astype(BF16)
     cross[...] = jnp.concatenate([crossed, crossed], axis=1)
-    loads[2].wait()
+    load_metric.wait()
     in_thirds(STEP_SIZE * metric[...], lane(0))
     picked_scale[...] = matmul(pick_wide[...], thirds[:, lane(0)])
-    loads[3].wait()
+    load_sources.wait()
     last = half - 2 + t
 
     def forward_level(i, carry):
@@ -556,8 +580,8 @@
 
     lax.fori_loop(0, half - 1 + t, forward_level, 0)
 
-    for load in loads[4:]:
-        load.wait()
+    load_weight.wait()
+    load_end.wait()
 
     @pl.when(t == 0)
     def _():
@@ -609,8 +633,6 @@
         send_ahead(levels - 1)
         reverse_far(levels - 2)
         split_field(adjoint)
-        state_copy(0).wait_recv()
-        reverse_near(0)
         pl.semaphore_wait(hello.at[2], 2)
         for r in range(1, plane):
             other = lax.rem(spot + r, plane)
@@ -631,6 +653,8 @@
             layer_copy(r, 0).start()
             if r > 0:
                 layer_copy(r, 1).start()
+        state_copy(0).wait_recv()
+        reverse_near(0)
         reverse_wait(levels - 1)
         reverse_far(levels - 1)
         end_copy.start()
@@ -657,8 +681,11 @@
     for s in range(1, layers):
         total = total + layer_parts[s]
     norm = math.sqrt(comps * nodes * blocks * n_space)
-    for n in range(levels):
-        grads[n] = STEP_SIZE * jnp.sum(total[n : n + 1, :]) / norm
+    sums = jnp.sum(total, axis=1, keepdims=True) * (STEP_SIZE / norm)
+    diagonal = lax.broadcasted_iota(jnp.int32, (levels, nodes), 1) == row_of
+    grads_row[...] = jnp.sum(jnp.where(diagonal, sums, 0.0), axis=0, keepdims=True)
+    give_sums = pltpu.make_async_copy(grads_row, grads, out_sem.at[1])
+    give_sums.start()
 
     def drain(i, carry):
         for d, offset in enumerate(OFFSETS):
@@ -704,6 +731,8 @@
             layer_copy(r, 0).wait_send()
             if r > 0:
                 layer_copy(r, 1).wait_send()
+
+    give_sums.wait()
 
 
 def solution(mesh):
@@ -725,7 +754,13 @@
         vmem = pltpu.VMEM
         dma = pltpu.SemaphoreType.DMA
         field = (comps, blocks, nodes)
+        smem = pltpu.SMEM
         scratch = [
+            smem((levels,), F32),
+            smem(mixing.shape, F32),
+            vmem((links, blocks), jnp.int32),
+            smem(send_idx.shape, jnp.int32),
+            vmem((1, nodes), F32),
             vmem((levels + 1, *field), F32),
             vmem((2, *field), F32),
             vmem((blocks, nodes), F32),
@@ -774,7 +809,7 @@
             vmem((plane, levels, nodes), F32),
             vmem((levels, nodes), F32),
             vmem((layers, levels, nodes), F32),
-            dma((6,)),
+            dma((10,)),
             dma((half, 4)),
             dma((half, 4)),
             dma((levels, 4)),
@@ -789,36 +824,25 @@
             dma((2, layers)),
             dma((layers,)),
             dma((2,)),
-            dma,
+            dma((2,)),
             pltpu.SemaphoreType.REGULAR((3,)),
         ]
         anywhere = pl.BlockSpec(memory_space=pl.ANY)
-        scalars = pl.BlockSpec(memory_space=pltpu.SMEM)
-        return pl.pallas_call(
+        results, sums = pl.pallas_call(
             functools.partial(sweep, n_space, plane),
             out_shape=(
                 jax.ShapeDtypeStruct((1, *field), F32),
-                jax.ShapeDtypeStruct((levels,), F32),
+                jax.ShapeDtypeStruct((1, nodes), F32),
             ),
-            in_specs=[
-                anywhere,
-                anywhere,
-                scalars,
-                anywhere,
-                anywhere,
-                anywhere,
-                anywhere,
-                scalars,
-                pl.BlockSpec(memory_space=pltpu.VMEM),
-                scalars,
-            ],
-            out_specs=(anywhere, scalars),
+            in_specs=[pl.BlockSpec(memory_space=pltpu.HBM)] * 10,
+            out_specs=(anywhere, anywhere),
             scratch_shapes=scratch,
             compiler_params=pltpu.CompilerParams(
                 collective_id=0, has_side_effects=True, vmem_limit_bytes=67043328
             ),
             name="adjoint_window",
         )(checkpoints, sources, pitch, metric, obj_weight, adjoint_end, lift, mixing, faces.T, send_idx)
+        return results, sums[0, :levels]
 
     return jax.shard_map(
         shards,

time: 84 us -> 82.1 us (0.977)
  Pallas kernels: 81 us -> 78.4 us
    pallas_call x1, Pallas kernels: 81 us -> 78.4 us  [shards(): pl.pallas_call(functools.partial(sweep, n_space, plane), out_shape=(jax.S...]
    unnamed x4 -> x3, local copies, waits for them, and re-layouts: 2.23 us -> 2.32 us
where the time goes in v5:
time: 82.1 us; the launch traced here: 81.9 us
  Pallas kernels  78.4 us (95%)
  local copies, waits for them, and re-layouts  2.83 us (3%)
    pallas_call x1, Pallas kernels, shards(): pl.pallas_call(functools.partial(sweep, n_space, plane), out_shape=(jax.S...  78.4 us
    unnamed x3, local copies, waits for them, and re-layouts  2.32 us

profile of v5, /device:TPU:1, one launch (start us, length us, event | category | flops | bytes accessed | tf_op | source)
XLA Modules:
  0.0 81.9 jit_solution(10539898389901384934)
XLA Ops:
  0.6 78.4 %adjoint_window.1 = (f32[1,5,128,128]{3,2,1,0:T(8,128)}, f32[1,128]{1,0:T(1,128)}) custom-call(f32[1,5,128,128]{3,2,1,0:T(8,128)} %checkpoint_in.1, f32[2,5,128,128]{3,2,1,0:T(8,128)} %sources_in.1, f32[8]{0:T(128)} %pitch_in.1, f32[128,128]{1,0:T(8,128)} %metric_in.1, f32[5,128,128]{2,1,0:T(8,128)} %weight_in.1, f32[5,128,128]{2,1,0:T(8,128)} %end_in.1, ...), custom_call_target="tpu_custom_call" | custom-call | tf_op jit(solution)/shard_map/adjoint_window/pallas_call | solution.py:831
  79.1 0.0 copy-start
  79.1 0.6 copy-done
  79.7 0.5 slice_bitcast_fusion
  80.2 1.7 %copy.13 = f32[1,5,128,128]{3,2,1,0:T(8,128)} copy(f32[1,5,128,128]{3,2,1,0:T(8,128)} %get-tuple-element.8) | data formatting | bytes 655360
Async XLA Ops:
  79.1 0.6 copy-start

commit v6 on v5

--- a/solution.py
+++ b/solution.py
@@ -14,6 +14,7 @@
 MESH = pl.DeviceIdType.MESH
 F32, BF16 = jnp.float32, jnp.bfloat16
 CHUNK = 32
+FAR_HALF_FIRST = (32, 0)
 
 
 def matmul(left, right):
@@ -351,15 +352,17 @@
         picked[...] = matmul(pick_wide[...], thirds[...])
 
     def send_picked(i):
-        change = matmul(far_pick[...], halo_mixed[...])
         wide_scale = jnp.concatenate([picked_scale[...]] * comps, axis=1)
-        packets = jnp.tanh(picked[...] - wide_scale * change).astype(BF16)
-        for d in FARTHEST_FIRST:
-            fwd_out[i, d] = packets[d * halo : (d + 1) * halo]
-
-            @pl.when(exists(p + OFFSETS[d]))
-            def _():
-                fwd_copy(i, d, p + OFFSETS[d]).start()
+        for start in FAR_HALF_FIRST:
+            some = slice(start, start + CHUNK)
+            change = matmul(far_pick[some], halo_mixed[...])
+            packets = jnp.tanh(picked[some] - wide_scale[some] * change).astype(BF16)
+            for d in range(start // halo, (start + CHUNK) // halo):
+                fwd_out[i, d] = packets[d * halo - start : (d + 1) * halo - start]
+
+                @pl.when(exists(p + OFFSETS[d]))
+                def _():
+                    fwd_copy(i, d, p + OFFSETS[d]).start()
 
     def forward_end(i):
         scale = STEP_SIZE * metric[...]
@@ -371,28 +374,30 @@
         for e in range(comps):
             in_halves(metric[...] * field[e], split, lane(e))
 
-    def far_product():
+    def far_product(start):
         for k in range(1, slots):
-            for start in range(0, ghosts, CHUNK):
-                row = (k - 1) * ghosts + start
-                totals = [None] * comps
-                for e in range(comps):
-                    term = halo_pulled[row : row + CHUNK, lane(e)]
-                    for c in range(comps):
-                        more = mixing[k, e, c] * term
-                        totals[c] = more if totals[c] is None else totals[c] + more
+            row = (k - 1) * ghosts + start
+            totals = [None] * comps
+            for e in range(comps):
+                term = halo_pulled[row : row + CHUNK, lane(e)]
                 for c in range(comps):
-                    far_mixed[c * ghosts + start : c * ghosts + start + CHUNK, lane(k - 1)] = totals[
-                        c
-                    ].astype(BF16)
+                    more = mixing[k, e, c] * term
+                    totals[c] = more if totals[c] is None else totals[c] + more
+            for c in range(comps):
+                far_mixed[c * ghosts + start : c * ghosts + start + CHUNK, lane(k - 1)] = totals[
+                    c
+                ].astype(BF16)
+        left = jnp.concatenate(
+            [far_mixed[c * ghosts + start : c * ghosts + start + CHUNK] for c in range(comps)], axis=0
+        )
         right = jnp.concatenate([lift[k] for k in range(1, slots)], axis=0)
-        return matmul(far_mixed[...], right)
-
-    def ship_reverse(j, product):
+        return matmul(left, right)
+
+    def ship_reverse(j, start, product):
         packets = product.astype(BF16)
-        for d in FARTHEST_FIRST:
+        for d in range(start // halo, (start + CHUNK) // halo):
             for c in range(comps):
-                row = c * ghosts + d * halo
+                row = c * CHUNK + d * halo - start
                 rev_out[j, d, :, lane(c)] = packets[row : row + halo]
 
             @pl.when(exists(p - OFFSETS[d]))
@@ -401,21 +406,34 @@
 
     def send_reverse(j):
         halo_pulled[...] = matmul(far_t[...], split[...])
-        ship_reverse(j, far_product())
+        for start in FAR_HALF_FIRST:
+            ship_reverse(j, start, far_product(start))
 
     def reverse_ahead():
         split_field(slope)
         gain[...] = matmul(pick_wide[:, : 2 * blocks], split[...])
         split_field(base)
         halo_pulled[...] = matmul(far_t[...], split[...])
-        ahead[...] = far_product()
+        for start in FAR_HALF_FIRST:
+            product = far_product(start)
+            for c in range(comps):
+                row = c * ghosts + start
+                ahead[row : row + CHUNK] = product[c * CHUNK : (c + 1) * CHUNK]
 
     def send_ahead(j):
         for c in range(comps):
             back = jnp.concatenate([rev_in[j - 1, d, :, lane(c)] for d in range(4)], axis=0)
             in_halves(gain[:, lane(c)] * back.astype(F32), back_split, lane(c))
-        halo_pulled[...] = matmul(cross[...], back_split[...])
-        ship_reverse(j, ahead[...] - far_product())
+        for start in FAR_HALF_FIRST:
+            rows = [slice(k * ghosts + start, k * ghosts + start + CHUNK) for k in range(slots - 1)]
+            left = jnp.concatenate([cross[some] for some in rows], axis=0)
+            product = matmul(left, back_split[...])
+            for k, some in enumerate(rows):
+                halo_pulled[some] = product[k * CHUNK : (k + 1) * CHUNK]
+            made = jnp.concatenate(
+                [ahead[c * ghosts + start : c * ghosts + start + CHUNK] for c in range(comps)], axis=0
+            )
+            ship_reverse(j, start, made - far_product(start))
 
     def reverse_sum(n, field):
         by_cosine = jnp.zeros((8, nodes), F32)
@@ -500,6 +518,14 @@
             for c in range(comps):
                 sent += both[:, lane(c)]
         partial[0:1, :] = partial[0:1, :] - jnp.sum(sent, axis=0, keepdims=True)
+
+    norm = math.sqrt(comps * nodes * blocks * n_space)
+
+    def in_row(tile):
+        sums = jnp.sum(tile, axis=1, keepdims=True) * (STEP_SIZE / norm)
+        lanes = lax.broadcasted_iota(jnp.int32, (levels, nodes), 1)
+        diagonal = lanes == lax.broadcasted_iota(jnp.int32, (levels, nodes), 0)
+        return jnp.sum(jnp.where(diagonal, sums, 0.0), axis=0, keepdims=True)
 
     load_first.wait()
     squash(lambda c: states[first, c])
@@ -647,8 +673,9 @@
         total = plane_parts[0]
         for s in range(1, plane):
             total = total + plane_parts[s]
-        plane_sum[...] = total
-        layer_parts[layer] = total
+        row = in_row(total)
+        plane_sum[...] = row
+        layer_parts[layer] = row
         for r in range(layers):
             layer_copy(r, 0).start()
             if r > 0:
@@ -658,6 +685,49 @@
         reverse_wait(levels - 1)
         reverse_far(levels - 1)
         end_copy.start()
+
+    def drain(i, carry):
+        for d, offset in enumerate(OFFSETS):
+
+            @pl.when(exists(p + offset))
+            def _():
+                fwd_copy(i, d, p).wait_send()
+
+        return carry
+
+    lax.fori_loop(0, half - 1 + t, drain, 0)
+
+    @pl.when(t == 0)
+    def _():
+        for i in range(half):
+            state_copy(i).wait_send()
+        for d, offset in enumerate(OFFSETS):
+
+            @pl.when(exists(p + offset))
+            def _():
+                bend_copy(d, p).wait_send()
+
+        bend_pass.wait_send()
+
+    @pl.when(t == 1)
+    def _():
+        def drain_reverse(j, carry):
+            for d, offset in enumerate(OFFSETS):
+
+                @pl.when(exists(p - offset))
+                def _():
+                    rev_copy(j, d, p).wait_send()
+
+            return carry
+
+        lax.fori_loop(0, levels, drain_reverse, 0)
+        keep_copy.wait()
+        for r in range(1, plane):
+            plane_copy(r).wait_send()
+        for r in range(layers):
+            layer_copy(r, 0).wait_send()
+            if r > 0:
+                layer_copy(r, 1).wait_send()
 
     def layer_wait(r):
         other = lax.rem(layer + r, layers)
@@ -680,59 +750,39 @@
     total = layer_parts[0]
     for s in range(1, layers):
         total = total + layer_parts[s]
-    norm = math.sqrt(comps * nodes * blocks * n_space)
-    sums = jnp.sum(total, axis=1, keepdims=True) * (STEP_SIZE / norm)
-    diagonal = lax.broadcasted_iota(jnp.int32, (levels, nodes), 1) == row_of
-    grads_row[...] = jnp.sum(jnp.where(diagonal, sums, 0.0), axis=0, keepdims=True)
+    grads_row[...] = total
     give_sums = pltpu.make_async_copy(grads_row, grads, out_sem.at[1])
     give_sums.start()
-
-    def drain(i, carry):
-        for d, offset in enumerate(OFFSETS):
-
-            @pl.when(exists(p + offset))
-            def _():
-                fwd_copy(i, d, p).wait_send()
-
-        return carry
-
-    lax.fori_loop(0, half - 1 + t, drain, 0)
 
     @pl.when(t == 0)
     def _():
         end_copy.wait_recv()
-        for i in range(half):
-            state_copy(i).wait_send()
-        for d, offset in enumerate(OFFSETS):
-
-            @pl.when(exists(p + offset))
-            def _():
-                bend_copy(d, p).wait_send()
-
-        bend_pass.wait_send()
 
     @pl.when(t == 1)
     def _():
-        def drain_reverse(j, carry):
-            for d, offset in enumerate(OFFSETS):
-
-                @pl.when(exists(p - offset))
-                def _():
-                    rev_copy(j, d, p).wait_send()
-
-            return carry
-
-        lax.fori_loop(0, levels, drain_reverse, 0)
-        keep_copy.wait()
         end_copy.wait_send()
-        for r in range(1, plane):
-            plane_copy(r).wait_send()
-        for r in range(layers):
-            layer_copy(r, 0).wait_send()
-            if r > 0:
-                layer_copy(r, 1).wait_send()
 
     give_sums.wait()
+
+
+def deliver(found, row, bounds, grads, held, sums, sums_out, sem):
+    comps = held.shape[0]
+    into = [pltpu.make_async_copy(found.at[0, c], held.at[c], sem.at[0, c]) for c in range(comps)]
+    outof = [pltpu.make_async_copy(held.at[c], bounds.at[0, c], sem.at[1, c]) for c in range(comps)]
+    row_in = pltpu.make_async_copy(row, sums, sem.at[0, comps])
+    row_out = pltpu.make_async_copy(sums_out, grads, sem.at[1, comps])
+    row_in.start()
+    for copy in into:
+        copy.start()
+    row_in.wait()
+    sums_out[...] = sums[0, : sums_out.shape[0]]
+    row_out.start()
+    for arrive, leave in zip(into, outof):
+        arrive.wait()
+        leave.start()
+    row_out.wait()
+    for leave in outof:
+        leave.wait()
 
 
 def solution(mesh):
@@ -807,8 +857,8 @@
             vmem((4, halo, wide), BF16),
             vmem((levels, nodes), F32),
             vmem((plane, levels, nodes), F32),
-            vmem((levels, nodes), F32),
-            vmem((layers, levels, nodes), F32),
+            vmem((1, nodes), F32),
+            vmem((layers, 1, nodes), F32),
             dma((10,)),
             dma((half, 4)),
             dma((half, 4)),
@@ -842,7 +892,23 @@
             ),
             name="adjoint_window",
         )(checkpoints, sources, pitch, metric, obj_weight, adjoint_end, lift, mixing, faces.T, send_idx)
-        return results, sums[0, :levels]
+        return pl.pallas_call(
+            deliver,
+            out_shape=(
+                jax.ShapeDtypeStruct((1, *field), F32),
+                jax.ShapeDtypeStruct((levels,), F32),
+            ),
+            in_specs=[anywhere, anywhere],
+            out_specs=(anywhere, anywhere),
+            scratch_shapes=[
+                vmem(field, F32),
+                vmem((1, nodes), F32),
+                vmem((levels,), F32),
+                dma((2, comps + 1)),
+            ],
+            compiler_params=pltpu.CompilerParams(vmem_limit_bytes=67043328),
+            name="deliver",
+        )(results, sums)
 
     return jax.shard_map(
         shards,

time: 82.1 us -> 80.1 us (0.976)
  local copies, waits for them, and re-layouts: 2.83 us -> 0 us
  Pallas kernels: 78.4 us -> 79.3 us
    unnamed x3 -> x0, local copies, waits for them, and re-layouts: 2.32 us -> none
    pallas_call x0 -> x1, Pallas kernels: none -> 1.7 us  [shards(): pl.pallas_call(deliver, out_shape=(jax.ShapeDtypeStruct((1, *field), F32)...]
where the time goes in v6:
time: 80.1 us; the launch traced here: 80 us
  Pallas kernels  79.3 us (99%)
    pallas_call x1, Pallas kernels, shards(): pl.pallas_call(functools.partial(sweep, n_space, plane), out_shape=(jax.S...  77.6 us
    pallas_call x1, Pallas kernels, shards(): pl.pallas_call(deliver, out_shape=(jax.ShapeDtypeStruct((1, *field), F32)...  1.7 us

profile of v6, /device:TPU:1, one launch (start us, length us, event | category | flops | bytes accessed | tf_op | source)
XLA Modules:
  0.0 80.0 jit_solution(4228702601896284170)
XLA Ops:
  0.6 77.6 %adjoint_window.1 = (f32[1,5,128,128]{3,2,1,0:T(8,128)}, f32[1,128]{1,0:T(1,128)}) custom-call(f32[1,5,128,128]{3,2,1,0:T(8,128)} %checkpoint_in.1, f32[2,5,128,128]{3,2,1,0:T(8,128)} %sources_in.1, f32[8]{0:T(128)} %pitch_in.1, f32[128,128]{1,0:T(8,128)} %metric_in.1, f32[5,128,128]{2,1,0:T(8,128)} %weight_in.1, f32[5,128,128]{2,1,0:T(8,128)} %end_in.1, ...), custom_call_target="tpu_custom_call" | custom-call | tf_op jit(solution)/shard_map/adjoint_window/pallas_call | solution.py:881
  78.3 1.7 %deliver.1 = (f32[1,5,128,128]{3,2,1,0:T(8,128)}, f32[8]{0:T(128)}) custom-call(f32[1,5,128,128]{3,2,1,0:T(8,128)} %get-tuple-element.4.found, f32[1,128]{1,0:T(1,128)} %get-tuple-element.5.row), custom_call_target="tpu_custom_call" | custom-call | tf_op jit(solution)/shard_map/deliver/pallas_call | solution.py:895

commit v7 on v6

--- a/solution.py
+++ b/solution.py
@@ -19,6 +19,10 @@
 
 def matmul(left, right):
     return jnp.dot(left, right, preferred_element_type=F32)
+
+
+def parity(level):
+    return level % 2 if isinstance(level, int) else lax.rem(level, 2)
 
 
 def sweep(
@@ -203,8 +207,8 @@
         return pltpu.make_async_remote_copy(
             src_ref=fwd_out.at[i, d],
             dst_ref=fwd_in.at[i, d],
-            send_sem=fwd_send.at[i, d],
-            recv_sem=fwd_recv.at[i, d],
+            send_sem=fwd_send.at[parity(i), d],
+            recv_sem=fwd_recv.at[parity(i), d],
             device_id=(t, device),
             device_id_type=MESH,
         )
@@ -213,8 +217,8 @@
         return pltpu.make_async_remote_copy(
             src_ref=rev_out.at[i, d],
             dst_ref=rev_in.at[i, d],
-            send_sem=rev_send.at[i, d],
-            recv_sem=rev_recv.at[i, d],
+            send_sem=rev_send.at[parity(i), d],
+            recv_sem=rev_recv.at[parity(i), d],
             device_id=(t, device),
             device_id_type=MESH,
         )
@@ -243,8 +247,8 @@
         return pltpu.make_async_remote_copy(
             src_ref=partial,
             dst_ref=plane_parts.at[spot],
-            send_sem=plane_send.at[r],
-            recv_sem=plane_recv.at[spot],
+            send_sem=plane_send,
+            recv_sem=plane_recv,
             device_id=(1, layer * plane + lax.rem(spot + r, plane)),
             device_id_type=MESH,
         )
@@ -253,8 +257,8 @@
         return pltpu.make_async_remote_copy(
             src_ref=plane_sum,
             dst_ref=layer_parts.at[layer],
-            send_sem=layer_send.at[core, r],
-            recv_sem=layer_recv.at[layer],
+            send_sem=layer_send,
+            recv_sem=layer_recv,
             device_id=(core, lax.rem(layer + r, layers) * plane + spot),
             device_id_type=MESH,
         )
@@ -267,6 +271,16 @@
         device_id=(1 - t, p),
         device_id_type=MESH,
     )
+    def all_parts(parts, count, send_sem, recv_sem):
+        return pltpu.make_async_remote_copy(
+            src_ref=parts.at[pl.ds(0, count)],
+            dst_ref=parts.at[pl.ds(0, count)],
+            send_sem=send_sem,
+            recv_sem=recv_sem,
+            device_id=(1 - t, p),
+            device_id_type=MESH,
+        )
+
     end_copy = pltpu.make_async_remote_copy(
         src_ref=adjoint,
         dst_ref=bounds.at[0],
@@ -276,6 +290,20 @@
         device_id_type=MESH,
     )
     keep_copy = pltpu.make_async_copy(kept, bounds.at[0], out_sem.at[0])
+
+    def fwd_sent(i):
+        for d, offset in enumerate(OFFSETS):
+
+            @pl.when(exists(p + offset))
+            def _():
+                fwd_copy(i, d, p).wait_send()
+
+    def rev_sent(j):
+        for d, offset in enumerate(OFFSETS):
+
+            @pl.when(exists(p - offset))
+            def _():
+                rev_copy(j, d, p).wait_send()
 
     def in_halves(value, where, columns):
         rows = value.shape[0]
@@ -586,6 +614,11 @@
     def forward_level(i, carry):
         forward_near(i)
         forward_ahead()
+
+        @pl.when(i > 0)
+        def _():
+            fwd_sent(i - 1)
+
         forward_far(i)
 
         @pl.when(i < last)
@@ -632,6 +665,11 @@
             reverse_sum(n, adjoint)
             reverse_near(n)
             reverse_ahead()
+
+            @pl.when(j > 0)
+            def _():
+                rev_sent(j - 1)
+
             reverse_wait(j)
             send_ahead(j + 1)
             reverse_far(j)
@@ -655,21 +693,13 @@
         for r in range(1, plane):
             plane_copy(r).start()
         reverse_ahead()
+        rev_sent(levels - 3)
         reverse_wait(levels - 2)
         send_ahead(levels - 1)
         reverse_far(levels - 2)
         split_field(adjoint)
         pl.semaphore_wait(hello.at[2], 2)
-        for r in range(1, plane):
-            other = lax.rem(spot + r, plane)
-            pltpu.make_async_remote_copy(
-                src_ref=partial,
-                dst_ref=plane_parts.at[other],
-                send_sem=plane_send.at[r],
-                recv_sem=plane_recv.at[other],
-                device_id=(1, p),
-                device_id_type=MESH,
-            ).wait_recv()
+        all_parts(plane_parts, plane - 1, plane_send, plane_recv).wait_recv()
         total = plane_parts[0]
         for s in range(1, plane):
             total = total + plane_parts[s]
@@ -682,20 +712,12 @@
                 layer_copy(r, 1).start()
         state_copy(0).wait_recv()
         reverse_near(0)
+        rev_sent(levels - 2)
         reverse_wait(levels - 1)
         reverse_far(levels - 1)
         end_copy.start()
 
-    def drain(i, carry):
-        for d, offset in enumerate(OFFSETS):
-
-            @pl.when(exists(p + offset))
-            def _():
-                fwd_copy(i, d, p).wait_send()
-
-        return carry
-
-    lax.fori_loop(0, half - 1 + t, drain, 0)
+    fwd_sent(last)
 
     @pl.when(t == 0)
     def _():
@@ -711,41 +733,18 @@
 
     @pl.when(t == 1)
     def _():
-        def drain_reverse(j, carry):
-            for d, offset in enumerate(OFFSETS):
-
-                @pl.when(exists(p - offset))
-                def _():
-                    rev_copy(j, d, p).wait_send()
-
-            return carry
-
-        lax.fori_loop(0, levels, drain_reverse, 0)
+        rev_sent(levels - 1)
         keep_copy.wait()
-        for r in range(1, plane):
-            plane_copy(r).wait_send()
-        for r in range(layers):
-            layer_copy(r, 0).wait_send()
-            if r > 0:
-                layer_copy(r, 1).wait_send()
-
-    def layer_wait(r):
-        other = lax.rem(layer + r, layers)
-        pltpu.make_async_remote_copy(
-            src_ref=plane_sum,
-            dst_ref=layer_parts.at[other],
-            send_sem=layer_send.at[0, r],
-            recv_sem=layer_recv.at[other],
-            device_id=(1 - t, p),
-            device_id_type=MESH,
-        ).wait_recv()
-
-    for r in range(1, layers):
-        layer_wait(r)
+        all_parts(plane_parts, plane - 1, plane_send, plane_recv).wait_send()
+        all_parts(layer_parts, 2 * layers - 1, layer_send, layer_recv).wait_send()
 
     @pl.when(t == 0)
     def _():
-        layer_wait(0)
+        all_parts(layer_parts, layers, layer_send, layer_recv).wait_recv()
+
+    @pl.when(t == 1)
+    def _():
+        all_parts(layer_parts, layers - 1, layer_send, layer_recv).wait_recv()
 
     total = layer_parts[0]
     for s in range(1, layers):
@@ -858,21 +857,21 @@
             vmem((levels, nodes), F32),
             vmem((plane, levels, nodes), F32),
             vmem((1, nodes), F32),
-            vmem((layers, 1, nodes), F32),
+            vmem((2 * layers, 1, nodes), F32),
             dma((10,)),
-            dma((half, 4)),
-            dma((half, 4)),
-            dma((levels, 4)),
-            dma((levels, 4)),
+            dma((2, 4)),
+            dma((2, 4)),
+            dma((2, 4)),
+            dma((2, 4)),
             dma((4,)),
             dma((4,)),
             dma((2,)),
             dma((half,)),
             dma((half,)),
-            dma((plane,)),
-            dma((plane,)),
-            dma((2, layers)),
-            dma((layers,)),
+            dma,
+            dma,
+            dma,
+            dma,
             dma((2,)),
             dma((2,)),
             pltpu.SemaphoreType.REGULAR((3,)),

time: 80.1 us -> 79 us (0.986)
  Pallas kernels: 79.3 us -> 78.2 us
    pallas_call x1, Pallas kernels: 77.6 us -> 76.5 us  [shards(): pl.pallas_call(functools.partial(sweep, n_space, plane), out_shape=(jax.S...]
where the time goes in v7:
time: 79 us; the launch traced here: 78.9 us
  Pallas kernels  78.2 us (99%)
    pallas_call x1, Pallas kernels, shards(): pl.pallas_call(functools.partial(sweep, n_space, plane), out_shape=(jax.S...  76.5 us
    pallas_call x1, Pallas kernels, shards(): pl.pallas_call(deliver, out_shape=(jax.ShapeDtypeStruct((1, *field), F32)...  1.7 us

profile of v7, /device:TPU:1, one launch (start us, length us, event | category | flops | bytes accessed | tf_op | source)
XLA Modules:
  0.0 78.9 jit_solution(17422417236984757821)
XLA Ops:
  0.6 76.5 %adjoint_window.1 = (f32[1,5,128,128]{3,2,1,0:T(8,128)}, f32[1,128]{1,0:T(1,128)}) custom-call(f32[1,5,128,128]{3,2,1,0:T(8,128)} %checkpoint_in.1, f32[2,5,128,128]{3,2,1,0:T(8,128)} %sources_in.1, f32[8]{0:T(128)} %pitch_in.1, f32[128,128]{1,0:T(8,128)} %metric_in.1, f32[5,128,128]{2,1,0:T(8,128)} %weight_in.1, f32[5,128,128]{2,1,0:T(8,128)} %end_in.1, ...), custom_call_target="tpu_custom_call" | custom-call | tf_op jit(solution)/shard_map/adjoint_window/pallas_call | solution.py:880
  77.1 1.7 %deliver.1 = (f32[1,5,128,128]{3,2,1,0:T(8,128)}, f32[8]{0:T(128)}) custom-call(f32[1,5,128,128]{3,2,1,0:T(8,128)} %get-tuple-element.4.found, f32[1,128]{1,0:T(1,128)} %get-tuple-element.5.row), custom_call_target="tpu_custom_call" | custom-call | tf_op jit(solution)/shard_map/deliver/pallas_call | solution.py:894

commit v8 on v7

--- a/solution.py
+++ b/solution.py
@@ -124,6 +124,12 @@
     layer = p // plane
     first = t * half
 
+    hot = jnp.where(lax.rem(p, 4) >= 2, 1, 0)
+    toward = 2 * hot - 1
+    aim = (-2 * toward, -toward, 2 * toward, toward)
+    pull_way = (2 + hot, hot, 3 - hot, 1 - hot)
+    back_way = (3 - hot, 1 - hot, 2 + hot, hot)
+
     def exists(q):
         return jnp.logical_and(q >= 0, q < n_space)
 
@@ -188,7 +194,7 @@
     for d in range(4):
         for s in range(halo):
             row = d * halo + s
-            pick[pl.ds(row, 1), :] = jnp.where(lane_of == send_idx[0, d, s], 1.0, 0.0)
+            pick[pl.ds(row, 1), :] = jnp.where(lane_of == send_idx[0, pull_way[d], s], 1.0, 0.0)
 
     for d, offset in enumerate(OFFSETS):
 
@@ -203,31 +209,31 @@
             for i in range(levels):
                 rev_in[i, d] = jnp.zeros(rev_in.shape[2:], BF16)
 
-    def fwd_copy(i, d, device):
+    def fwd_copy(i, d, device, q=0):
         return pltpu.make_async_remote_copy(
-            src_ref=fwd_out.at[i, d],
+            src_ref=fwd_out.at[i, q],
             dst_ref=fwd_in.at[i, d],
-            send_sem=fwd_send.at[parity(i), d],
+            send_sem=fwd_send.at[parity(i), q],
             recv_sem=fwd_recv.at[parity(i), d],
             device_id=(t, device),
             device_id_type=MESH,
         )
 
-    def rev_copy(i, d, device):
+    def rev_copy(i, d, device, q=0):
         return pltpu.make_async_remote_copy(
-            src_ref=rev_out.at[i, d],
+            src_ref=rev_out.at[i, q],
             dst_ref=rev_in.at[i, d],
-            send_sem=rev_send.at[parity(i), d],
+            send_sem=rev_send.at[parity(i), q],
             recv_sem=rev_recv.at[parity(i), d],
             device_id=(t, device),
             device_id_type=MESH,
         )
 
-    def bend_copy(d, device):
+    def bend_copy(d, device, q=0):
         return pltpu.make_async_remote_copy(
-            src_ref=bend_out.at[d],
+            src_ref=bend_out.at[q],
             dst_ref=bend_in.at[d],
-            send_sem=bend_send.at[d],
+            send_sem=bend_send.at[q],
             recv_sem=bend_recv.at[d],
             device_id=(t, device),
             device_id_type=MESH,
@@ -292,18 +298,18 @@
     keep_copy = pltpu.make_async_copy(kept, bounds.at[0], out_sem.at[0])
 
     def fwd_sent(i):
-        for d, offset in enumerate(OFFSETS):
-
-            @pl.when(exists(p + offset))
-            def _():
-                fwd_copy(i, d, p).wait_send()
+        for q in range(4):
+
+            @pl.when(exists(p + aim[q]))
+            def _():
+                fwd_copy(i, pull_way[q], p, q).wait_send()
 
     def rev_sent(j):
-        for d, offset in enumerate(OFFSETS):
-
-            @pl.when(exists(p - offset))
-            def _():
-                rev_copy(j, d, p).wait_send()
+        for q in range(4):
+
+            @pl.when(exists(p + aim[q]))
+            def _():
+                rev_copy(j, back_way[q], p, q).wait_send()
 
     def in_halves(value, where, columns):
         rows = value.shape[0]
@@ -323,12 +329,12 @@
 
     def send_forward(i):
         packets = matmul(pick[...].astype(BF16), squashed[...]).astype(BF16)
-        for d in FARTHEST_FIRST:
-            fwd_out[i, d] = packets[d * halo : (d + 1) * halo]
-
-            @pl.when(exists(p + OFFSETS[d]))
-            def _():
-                fwd_copy(i, d, p + OFFSETS[d]).start()
+        for q in FARTHEST_FIRST:
+            fwd_out[i, q] = packets[q * halo : (q + 1) * halo]
+
+            @pl.when(exists(p + aim[q]))
+            def _():
+                fwd_copy(i, pull_way[q], p + aim[q], q).start()
 
     def forward_near(i):
         gathered[...] = matmul(near[...], squashed[...]).astype(BF16)
@@ -385,12 +391,12 @@
             some = slice(start, start + CHUNK)
             change = matmul(far_pick[some], halo_mixed[...])
             packets = jnp.tanh(picked[some] - wide_scale[some] * change).astype(BF16)
-            for d in range(start // halo, (start + CHUNK) // halo):
-                fwd_out[i, d] = packets[d * halo - start : (d + 1) * halo - start]
-
-                @pl.when(exists(p + OFFSETS[d]))
+            for q in range(start // halo, (start + CHUNK) // halo):
+                fwd_out[i, q] = packets[q * halo - start : (q + 1) * halo - start]
+
+                @pl.when(exists(p + aim[q]))
                 def _():
-                    fwd_copy(i, d, p + OFFSETS[d]).start()
+                    fwd_copy(i, pull_way[q], p + aim[q], q).start()
 
     def forward_end(i):
         scale = STEP_SIZE * metric[...]
@@ -423,14 +429,14 @@
 
     def ship_reverse(j, start, product):
         packets = product.astype(BF16)
-        for d in range(start // halo, (start + CHUNK) // halo):
+        for q in range(start // halo, (start + CHUNK) // halo):
             for c in range(comps):
-                row = c * CHUNK + d * halo - start
-                rev_out[j, d, :, lane(c)] = packets[row : row + halo]
-
-            @pl.when(exists(p - OFFSETS[d]))
-            def _():
-                rev_copy(j, d, p - OFFSETS[d]).start()
+                row = c * CHUNK + q * halo - start
+                rev_out[j, q, :, lane(c)] = packets[row : row + halo]
+
+            @pl.when(exists(p + aim[q]))
+            def _():
+                rev_copy(j, back_way[q], p + aim[q], q).start()
 
     def send_reverse(j):
         halo_pulled[...] = matmul(far_t[...], split[...])
@@ -450,7 +456,7 @@
 
     def send_ahead(j):
         for c in range(comps):
-            back = jnp.concatenate([rev_in[j - 1, d, :, lane(c)] for d in range(4)], axis=0)
+            back = jnp.concatenate([rev_in[j - 1, d, :, lane(c)] for d in pull_way], axis=0)
             in_halves(gain[:, lane(c)] * back.astype(F32), back_split, lane(c))
         for start in FAR_HALF_FIRST:
             rows = [slice(k * ghosts + start, k * ghosts + start + CHUNK) for k in range(slots - 1)]
@@ -511,7 +517,7 @@
                 rev_copy(j, d, p).wait_recv()
 
     def reverse_far(j):
-        ghost = jnp.concatenate([rev_in[j, d] for d in range(4)], axis=0)
+        ghost = jnp.concatenate([rev_in[j, d] for d in pull_way], axis=0)
         arrived = matmul(pick_t[...], ghost)
         for c in range(comps):
             adjoint[c] = base[c] - slope[c] * arrived[:, lane(c)]
@@ -522,12 +528,12 @@
             turning = cosines[0:1, :] * sources[1, e] - sines[0:1, :] * sources[0, e]
             squashed[:, lane(e)] = (STEP_SIZE * (1.0 - bent * bent) * turning).astype(BF16)
         packets = matmul(pick[...].astype(BF16), squashed[...]).astype(BF16)
-        for d, offset in enumerate(OFFSETS):
-            bend_out[d] = packets[d * halo : (d + 1) * halo]
-
-            @pl.when(exists(p + offset))
-            def _():
-                bend_copy(d, p + offset).start()
+        for q in range(4):
+            bend_out[q] = packets[q * halo : (q + 1) * halo]
+
+            @pl.when(exists(p + aim[q]))
+            def _():
+                bend_copy(pull_way[q], p + aim[q], q).start()
 
         for d, offset in enumerate(OFFSETS):
 
@@ -542,7 +548,7 @@
         bend_pass.wait_recv()
         sent = jnp.zeros((halo, nodes), F32)
         for d in range(4):
-            both = rev_out[j, d].astype(F32) * bend_there[d].astype(F32)
+            both = rev_out[j, d].astype(F32) * bend_there[back_way[d]].astype(F32)
             for c in range(comps):
                 sent += both[:, lane(c)]
         partial[0:1, :] = partial[0:1, :] - jnp.sum(sent, axis=0, keepdims=True)
@@ -590,13 +596,18 @@
         near_t[(k - 1) * blocks : k * blocks, :blocks] = turned
         near_t[(k - 1) * blocks : k * blocks, blocks:] = turned
     slot_at = lax.rem(row_at, ghosts)
+    group = slot_at // halo
+    way = jnp.where(group == 0, back_way[0], back_way[1])
+    way = jnp.where(group == 2, back_way[2], way)
+    way = jnp.where(group == 3, back_way[3], way)
+    sent_at = way * halo + lax.rem(slot_at, halo)
     for pair in range(2):
         upper = faces[2 * pair : 2 * pair + 1, :] - blocks
         lower = faces[2 * pair + 1 : 2 * pair + 2, :] - blocks
         wanted = jnp.where(row_at < ghosts, upper, lower)
         chosen = jnp.where(wanted == slot_at, 1.0, 0.0)
         far[:, pair * blocks : (pair + 1) * blocks] = chosen.T.astype(BF16)
-        turned = chosen.astype(BF16)
+        turned = jnp.where(wanted == sent_at, 1.0, 0.0).astype(BF16)
         far_t[pair * blocks : (pair + 1) * blocks, :blocks] = turned
         far_t[pair * blocks : (pair + 1) * blocks, blocks:] = turned
     wide_pick = pick[...].astype(BF16)
@@ -723,11 +734,11 @@
     def _():
         for i in range(half):
             state_copy(i).wait_send()
-        for d, offset in enumerate(OFFSETS):
-
-            @pl.when(exists(p + offset))
-            def _():
-                bend_copy(d, p).wait_send()
+        for q in range(4):
+
+            @pl.when(exists(p + aim[q]))
+            def _():
+                bend_copy(pull_way[q], p, q).wait_send()
 
         bend_pass.wait_send()
 

time: 79 us -> 78.1 us (0.989)
  Pallas kernels: 78.2 us -> 77.3 us
    pallas_call x1, Pallas kernels: 76.5 us -> 75.6 us  [shards(): pl.pallas_call(functools.partial(sweep, n_space, plane), out_shape=(jax.S...]
where the time goes in v8:
time: 78.1 us; the launch traced here: 77.9 us
  Pallas kernels  77.3 us (99%)
    pallas_call x1, Pallas kernels, shards(): pl.pallas_call(functools.partial(sweep, n_space, plane), out_shape=(jax.S...  75.6 us
    pallas_call x1, Pallas kernels, shards(): pl.pallas_call(deliver, out_shape=(jax.ShapeDtypeStruct((1, *field), F32)...  1.7 us

profile of v8, /device:TPU:1, one launch (start us, length us, event | category | flops | bytes accessed | tf_op | source)
XLA Modules:
  0.0 77.9 jit_solution(16010591540762931120)
XLA Ops:
  0.6 75.6 %adjoint_window.1 = (f32[1,5,128,128]{3,2,1,0:T(8,128)}, f32[1,128]{1,0:T(1,128)}) custom-call(f32[1,5,128,128]{3,2,1,0:T(8,128)} %checkpoint_in.1, f32[2,5,128,128]{3,2,1,0:T(8,128)} %sources_in.1, f32[8]{0:T(128)} %pitch_in.1, f32[128,128]{1,0:T(8,128)} %metric_in.1, f32[5,128,128]{2,1,0:T(8,128)} %weight_in.1, f32[5,128,128]{2,1,0:T(8,128)} %end_in.1, ...), custom_call_target="tpu_custom_call" | custom-call | tf_op jit(solution)/shard_map/adjoint_window/pallas_call | solution.py:891
  76.2 1.7 %deliver.1 = (f32[1,5,128,128]{3,2,1,0:T(8,128)}, f32[8]{0:T(128)}) custom-call(f32[1,5,128,128]{3,2,1,0:T(8,128)} %get-tuple-element.4.found, f32[1,128]{1,0:T(1,128)} %get-tuple-element.5.row), custom_call_target="tpu_custom_call" | custom-call | tf_op jit(solution)/shard_map/deliver/pallas_call | solution.py:905

commit v9 on v8

--- a/solution.py
+++ b/solution.py
@@ -90,6 +90,7 @@
     bend_in,
     bend_there,
     partial,
+    plane_row,
     plane_parts,
     plane_sum,
     layer_parts,
@@ -251,7 +252,7 @@
 
     def plane_copy(r):
         return pltpu.make_async_remote_copy(
-            src_ref=partial,
+            src_ref=plane_row,
             dst_ref=plane_parts.at[spot],
             send_sem=plane_send,
             recv_sem=plane_recv,
@@ -700,7 +701,9 @@
         pl.semaphore_wait(hello.at[1], 2)
         call(2, 2)
         last_sum(levels - 2)
-        plane_parts[spot] = partial[...]
+        row = in_row(partial[...])
+        plane_row[...] = row
+        plane_parts[spot] = row
         for r in range(1, plane):
             plane_copy(r).start()
         reverse_ahead()
@@ -714,9 +717,8 @@
         total = plane_parts[0]
         for s in range(1, plane):
             total = total + plane_parts[s]
-        row = in_row(total)
-        plane_sum[...] = row
-        layer_parts[layer] = row
+        plane_sum[...] = total
+        layer_parts[layer] = total
         for r in range(layers):
             layer_copy(r, 0).start()
             if r > 0:
@@ -866,7 +868,8 @@
             vmem((4, halo, wide), BF16),
             vmem((4, halo, wide), BF16),
             vmem((levels, nodes), F32),
-            vmem((plane, levels, nodes), F32),
+            vmem((1, nodes), F32),
+            vmem((plane, 1, nodes), F32),
             vmem((1, nodes), F32),
             vmem((2 * layers, 1, nodes), F32),
             dma((10,)),

time: 78.1 us -> 78 us (level)
  no operation moved by 1% of the time
where the time goes in v9:
time: 78 us; the launch traced here: 77.9 us
  Pallas kernels  77.2 us (99%)
    pallas_call x1, Pallas kernels, shards(): pl.pallas_call(functools.partial(sweep, n_space, plane), out_shape=(jax.S...  75.5 us
    pallas_call x1, Pallas kernels, shards(): pl.pallas_call(deliver, out_shape=(jax.ShapeDtypeStruct((1, *field), F32)...  1.7 us

profile of v9, /device:TPU:1, one launch (start us, length us, event | category | flops | bytes accessed | tf_op | source)
XLA Modules:
  0.0 77.9 jit_solution(10506554944480026223)
XLA Ops:
  0.6 75.5 %adjoint_window.1 = (f32[1,5,128,128]{3,2,1,0:T(8,128)}, f32[1,128]{1,0:T(1,128)}) custom-call(f32[1,5,128,128]{3,2,1,0:T(8,128)} %checkpoint_in.1, f32[2,5,128,128]{3,2,1,0:T(8,128)} %sources_in.1, f32[8]{0:T(128)} %pitch_in.1, f32[128,128]{1,0:T(8,128)} %metric_in.1, f32[5,128,128]{2,1,0:T(8,128)} %weight_in.1, f32[5,128,128]{2,1,0:T(8,128)} %end_in.1, ...), custom_call_target="tpu_custom_call" | custom-call | tf_op jit(solution)/shard_map/adjoint_window/pallas_call | solution.py:894
  76.2 1.7 %deliver.1 = (f32[1,5,128,128]{3,2,1,0:T(8,128)}, f32[8]{0:T(128)}) custom-call(f32[1,5,128,128]{3,2,1,0:T(8,128)} %get-tuple-element.4.found, f32[1,128]{1,0:T(1,128)} %get-tuple-element.5.row), custom_call_target="tpu_custom_call" | custom-call | tf_op jit(solution)/shard_map/deliver/pallas_call | solution.py:908

commit v10 on v9

--- a/solution.py
+++ b/solution.py
@@ -778,11 +778,10 @@
 
 
 def deliver(found, row, bounds, grads, held, sums, sums_out, sem):
-    comps = held.shape[0]
-    into = [pltpu.make_async_copy(found.at[0, c], held.at[c], sem.at[0, c]) for c in range(comps)]
-    outof = [pltpu.make_async_copy(held.at[c], bounds.at[0, c], sem.at[1, c]) for c in range(comps)]
-    row_in = pltpu.make_async_copy(row, sums, sem.at[0, comps])
-    row_out = pltpu.make_async_copy(sums_out, grads, sem.at[1, comps])
+    into = [pltpu.make_async_copy(found.at[0], held, sem.at[0, 0])]
+    outof = [pltpu.make_async_copy(held, bounds.at[0], sem.at[1, 0])]
+    row_in = pltpu.make_async_copy(row, sums, sem.at[0, 1])
+    row_out = pltpu.make_async_copy(sums_out, grads, sem.at[1, 1])
     row_in.start()
     for copy in into:
         copy.start()
@@ -917,7 +916,7 @@
                 vmem(field, F32),
                 vmem((1, nodes), F32),
                 vmem((levels,), F32),
-                dma((2, comps + 1)),
+                dma((2, 2)),
             ],
             compiler_params=pltpu.CompilerParams(vmem_limit_bytes=67043328),
             name="deliver",

time: 78 us -> 78 us (level)
  no operation moved by 1% of the time
where the time goes in v10:
time: 78 us; the launch traced here: 77.9 us
  Pallas kernels  77.3 us (99%)
    pallas_call x1, Pallas kernels, shards(): pl.pallas_call(functools.partial(sweep, n_space, plane), out_shape=(jax.S...  75.5 us
    pallas_call x1, Pallas kernels, shards(): pl.pallas_call(deliver, out_shape=(jax.ShapeDtypeStruct((1, *field), F32)...  1.74 us

profile of v10, /device:TPU:1, one launch (start us, length us, event | category | flops | bytes accessed | tf_op | source)
XLA Modules:
  0.0 77.9 jit_solution(3838253601573201466)
XLA Ops:
  0.6 75.5 %adjoint_window.1 = (f32[1,5,128,128]{3,2,1,0:T(8,128)}, f32[1,128]{1,0:T(1,128)}) custom-call(f32[1,5,128,128]{3,2,1,0:T(8,128)} %checkpoint_in.1, f32[2,5,128,128]{3,2,1,0:T(8,128)} %sources_in.1, f32[8]{0:T(128)} %pitch_in.1, f32[128,128]{1,0:T(8,128)} %metric_in.1, f32[5,128,128]{2,1,0:T(8,128)} %weight_in.1, f32[5,128,128]{2,1,0:T(8,128)} %end_in.1, ...), custom_call_target="tpu_custom_call" | custom-call | tf_op jit(solution)/shard_map/adjoint_window/pallas_call | solution.py:893
  76.2 1.7 %deliver.1 = (f32[1,5,128,128]{3,2,1,0:T(8,128)}, f32[8]{0:T(128)}) custom-call(f32[1,5,128,128]{3,2,1,0:T(8,128)} %get-tuple-element.4.found, f32[1,128]{1,0:T(1,128)} %get-tuple-element.5.row), custom_call_target="tpu_custom_call" | custom-call | tf_op jit(solution)/shard_map/deliver/pallas_call | solution.py:907
